TPU v7x, 128 devices: a whole 4x4x4 slice. The times are simulated.
128 devices in a mesh: rep: 1, r: 4 (over x), s: 32 (over y, z, core).
Axes of the slice: x: 4, y: 4, z: 4, core: 2. Of those that a mesh axis runs over, the one named last changes fastest.
Arguments:
- x: bfloat16 [128, 2048, 1280], P(('rep', 'r', 's'))
- dy: bfloat16 [128, 2048, 1280], P(('rep', 'r', 's'))
- w_gate: bfloat16 [2, 1280, 4352], P(None, 's')
- w_up: bfloat16 [2, 1280, 4352], P(None, 's')
- w_down: bfloat16 [2, 4352, 1280], P(None, 's')
Outputs:
- output 1: bfloat16 [128, 2048, 1280], P(('rep', 'r', 's'))
- output 2: bfloat16 [2, 1280, 4352], P('rep', 's')
- output 3: bfloat16 [2, 1280, 4352], P('rep', 's')
- output 4: bfloat16 [2, 4352, 1280], P('rep', 's')
All inputs are finite; a program needn't handle non-finite values.
Results may differ from a plain program's by a relative error of at most 0.018.
Values are sent between devices in bfloat16 or wider.
A program may use at most 1.5 GiB of HBM per device.

v0:
```python
import jax
import jax.numpy as jnp
from jax import lax
from jax.sharding import PartitionSpec as P

NAMES = ("w_gate", "w_up", "w_down")


def matmul(a, w):
    return jnp.dot(a, w, preferred_element_type=jnp.float32).astype(jnp.bfloat16)


def normed(h):
    wide = h.astype(jnp.float32)
    scale = lax.rsqrt(jnp.mean(wide**2, -1, keepdims=True) + 1e-6)
    return (wide * scale).astype(jnp.bfloat16)


def layer(h, w):
    a = normed(h)
    gate = jnp.dot(a, w["w_gate"], preferred_element_type=jnp.float32)
    up = jnp.dot(a, w["w_up"], preferred_element_type=jnp.float32)
    return h + matmul((jax.nn.silu(gate) * up).astype(jnp.bfloat16), w["w_down"])


def solution(mesh):
    def fetched(weights, number):
        return {name: lax.all_gather(w[number], "s", axis=0, tiled=True) for name, w in zip(NAMES, weights, strict=True)}

    def summed(term):
        return lax.psum(lax.psum_scatter(term, "s", scatter_dimension=0, tiled=True), "r")

    def step(x, dy, *weights):
        layers = weights[0].shape[0]
        h, inputs = x[0], []
        for number in range(layers):
            inputs.append(h)
            h = layer(h, fetched(weights, number))
        by_h, mine = dy[0], [None] * layers
        for number in reversed(range(layers)):
            _, back = jax.vjp(lambda w, h: layer(h, w), fetched(weights, number), inputs[number])
            by_w, by_h = back(by_h)
            mine[number] = [summed(by_w[name]) for name in NAMES]
        return (by_h[None], *(jnp.stack([mine[number][i] for number in range(layers)]) for i in range(3)))

    states, cut = P(("rep", "r", "s"), None, None), P(None, "s", None)
    return jax.shard_map(
        step,
        mesh=mesh,
        in_specs=(states, states) + (cut,) * 3,
        out_specs=(states,) + (P("rep", "s", None),) * 3,
        check_vma=False,
    )
```

profile of v0, /device:TPU:0, one launch (start us, length us, event | category | flops | bytes accessed | tf_op | source)
XLA Modules:
  0.0 1150.5 jit_solution(14315161901130089020)
XLA Ops:
  7.2 0.0 all-gather.13.cloned.1.call-start
  7.2 2.0 fusion.84
  9.2 0.0 all-gather.13.cloned.1.call-update
  9.2 0.0 all-gather.15.cloned.1.call-start
  9.3 2.0 fusion.86
  11.3 0.0 all-gather.17.cloned.1.call-start
  11.3 2.0 fusion.85
  13.3 0.0 all-gather.17.cloned.1.call-update
  13.3 0.0 all-gather.21.cloned.1.call-start
  13.4 0.5 all-gather.21.cloned.1.call-update
  13.9 0.0 all-gather.23.cloned.1.call-start
  14.0 0.5 all-gather.23.cloned.1.call-update
  14.5 0.0 all-gather.19.cloned.1.call-start
  14.6 0.5 all-gather.19.cloned.1.call-update
  15.1 0.0 reduce-scatter.17.cloned.1.call-start
  15.1 7.9 copy.10
  23.0 3.6 fusion.34
  26.6 0.6 copy-done
  27.2 8.0 copy.9
  35.2 37.3 %all-gather.13.cloned.1.call-done = bf16[1,1280,4352]{2,1,0:T(8,128)(2,1)} async-done(((bf16[1,40,4352]{2,1,0:T(8,128)(2,1)}), bf16[1,1280,4352]{2,1,0:T(8,128)(2,1)}) %all-gather.13.cloned.1.call-update) | async-done | bytes 11141136 | tf_op jit(solution)/shard_map/all_gather | solution.py:28
  72.5 32.1 %fusion.28 = f32[2048,4352]{1,0:T(8,128)} fusion(bf16[1,1280,4352]{2,1,0:T(8,128)(2,1)} %all-gather.13.cloned.1.call-done, bf16[1,2048,1280]{1,2,0:T(8,128)(2,1)} %copy.10, f32[2048]{0:T(1024)S(1)} %fusion.77), kind=kOutput, calls=%fused_computation.54 | convolution fusion | flops 22824878080 | bytes 52043776 | tf_op jit(solution)/shard_map/dot_general | solution.py:21
  104.6 28.8 %all-gather.15.cloned.1.call-done = bf16[1,1280,4352]{2,1,0:T(8,128)(2,1)} async-done(((bf16[1,40,4352]{2,1,0:T(8,128)(2,1)}), bf16[1,1280,4352]{2,1,0:T(8,128)(2,1)}) %all-gather.15.cloned.1.call-update) | async-done | bytes 11141136 | tf_op jit(solution)/shard_map/all_gather | solution.py:28
  133.4 43.3 %multiply_convert_fusion.1 = (bf16[2048,4352]{1,0:T(8,128)(2,1)}, f32[2048,4352]{1,0:T(8,128)}) fusion(f32[2048,4352]{1,0:T(8,128)} %fusion.28, bf16[1,1280,4352]{2,1,0:T(8,128)(2,1)} %all-gather.15.cloned.1.call-done, bf16[1,2048,1280]{1,2,0:T(8,128)(2,1)} %copy.10, f32[2048]{0:T(1024)S(1)} %fusion.77), kind=kOutput, calls=%fused_computation.13 | convolution fusion | flops 22878355456 | bytes 105521152 | tf_op jit(solution)/shard_map/dot_general | solution.py:22
  176.7 17.6 %all-gather.17.cloned.1.call-done = bf16[1,4352,1280]{2,1,0:T(8,128)(2,1)} async-done(((bf16[1,136,1280]{2,1,0:T(8,128)(2,1)}), bf16[1,4352,1280]{2,1,0:T(8,128)(2,1)}) %all-gather.17.cloned.1.call-update) | async-done | bytes 11141136 | tf_op jit(solution)/shard_map/all_gather | solution.py:28
  194.3 32.1 %fusion.37 = (f32[2048]{0:T(1024)S(1)}, bf16[2048,1280]{0,1:T(8,128)(2,1)}) fusion(bf16[2048,4352]{1,0:T(8,128)(2,1)} %get-tuple-element.20, bf16[1,4352,1280]{2,1,0:T(8,128)(2,1)} %all-gather.17.cloned.1.call-done, bf16[1,2048,1280]{1,2,0:T(8,128)(2,1)} %copy.10), kind=kOutput, calls=%fused_computation.63 | convolution fusion | flops 22830118912 | bytes 39460864 | tf_op jit(solution)/shard_map/dot_general | solution.py:10
  226.3 28.7 %all-gather.21.cloned.1.call-done = bf16[1,4352,1280]{2,1,0:T(8,128)(2,1)} async-done(((bf16[1,136,1280]{2,1,0:T(8,128)(2,1)}), bf16[1,4352,1280]{2,1,0:T(8,128)(2,1)}) %all-gather.21.cloned.1.call-update) | async-done | bytes 11141136 | tf_op jit(solution)/shard_map/all_gather | solution.py:28
  255.0 30.5 %convolution_convert_fusion.1 = bf16[2048,4352]{1,0:T(8,128)(2,1)} fusion(bf16[1,4352,1280]{2,1,0:T(8,128)(2,1)} %all-gather.21.cloned.1.call-done, bf16[1,2048,1280]{2,1,0:T(8,128)(2,1)} %param.6), kind=kOutput, calls=%fused_computation.23 | convolution fusion | flops 22825926656 | bytes 34209792 | tf_op jit(solution)/shard_map/transpose(jvp())/dot_general | solution.py:10
  285.5 30.8 %all-gather.23.cloned.1.call-done = bf16[1,1280,4352]{2,1,0:T(8,128)(2,1)} async-done(((bf16[1,40,4352]{2,1,0:T(8,128)(2,1)}), bf16[1,1280,4352]{2,1,0:T(8,128)(2,1)}) %all-gather.23.cloned.1.call-update) | async-done | bytes 11141136 | tf_op jit(solution)/shard_map/all_gather | solution.py:28
  316.3 32.6 %fusion.12 = f32[2048,4352]{1,0:T(8,128)} fusion(bf16[1,1280,4352]{2,1,0:T(8,128)(2,1)} %all-gather.23.cloned.1.call-done, bf16[2048,1280]{0,1:T(8,128)(2,1)} %get-tuple-element.23, f32[2048]{0:T(1024)S(1)} %fusion.78), kind=kOutput, calls=%fused_computation.38 | convolution fusion | flops 22824878080 | bytes 52043776 | tf_op jit(solution)/shard_map/jvp()/dot_general | solution.py:22
  348.9 28.7 %all-gather.19.cloned.1.call-done = bf16[1,1280,4352]{2,1,0:T(8,128)(2,1)} async-done(((bf16[1,40,4352]{2,1,0:T(8,128)(2,1)}), bf16[1,1280,4352]{2,1,0:T(8,128)(2,1)}) %all-gather.19.cloned.1.call-update) | async-done | bytes 11141136 | tf_op jit(solution)/shard_map/all_gather | solution.py:28
  377.6 51.1 %fusion.1 = (bf16[2048,4352]{1,0:T(8,128)(2,1)}, f32[2048,4352]{1,0:T(8,128)}) fusion(f32[2048,4352]{1,0:T(8,128)} %fusion.12, bf16[2048,4352]{1,0:T(8,128)(2,1)} %convolution_convert_fusion.1, bf16[1,1280,4352]{2,1,0:T(8,128)(2,1)} %all-gather.19.cloned.1.call-done, bf16[2048,1280]{0,1:T(8,128)(2,1)} %get-tuple-element.23, f32[2048]{0:T(1024)S(1)} %fusion.78), kind=kOutput, calls=%fused_computation.7 | convolution fusion | flops 22931832832 | bytes 123346944 | tf_op jit(solution)/shard_map/jvp()/dot_general | solution.py:21
  428.7 38.4 %convolution_convert_fusion.2 = bf16[4352,1280]{1,0:T(8,128)(2,1)} fusion(f32[2048,4352]{1,0:T(8,128)} %fusion.12, bf16[1,2048,1280]{2,1,0:T(8,128)(2,1)} %param.6, f32[2048,4352]{1,0:T(8,128)} %get-tuple-element.25), kind=kOutput, calls=%fused_computation.24 | convolution fusion | flops 22876061696 | bytes 87687168 | tf_op jit(solution)/shard_map/transpose(jvp())/dot_general | solution.py:10
  467.2 0.0 reduce-scatter.17.cloned.1.call-update
  467.2 0.0 reduce-scatter.15.cloned.1.call-start
  467.2 33.7 %fusion.49 = bf16[2048,1280]{0,1:T(8,128)(2,1)} fusion(bf16[1,1280,4352]{2,1,0:T(8,128)(2,1)} %all-gather.23.cloned.1.call-done, bf16[2048,4352]{1,0:T(8,128)(2,1)} %convolution_convert_fusion.1, f32[2048,4352]{1,0:T(8,128)} %get-tuple-element.25), kind=kOutput, calls=%fused_computation.69 | convolution fusion | flops 22873112576 | bytes 69861376 | tf_op jit(solution)/shard_map/transpose(jvp())/dot_general | solution.py:22
  501.0 33.0 %fusion.39 = (f32[2048]{0:T(1024)S(1)}, bf16[2048,1280]{0,1:T(8,128)(2,1)}) fusion(bf16[2048,1280]{0,1:T(8,128)(2,1)} %get-tuple-element.23, bf16[2048,1280]{0,1:T(8,128)(2,1)} %fusion.49, bf16[2048,4352]{1,0:T(8,128)(2,1)} %get-tuple-element.24, bf16[1,1280,4352]{2,1,0:T(8,128)(2,1)} %all-gather.19.cloned.1.call-done), kind=kOutput, calls=%fused_computation.65 | convolution fusion | flops 22830118912 | bytes 44703744 | tf_op jit(solution)/shard_map/transpose(jvp())/dot_general | solution.py:21
  534.1 12.3 %fusion.66 = bf16[2048,1280]{0,1:T(8,128)(2,1)} fusion(bf16[2048,1280]{0,1:T(8,128)(2,1)} %get-tuple-element.23, bf16[2048,1280]{0,1:T(8,128)(2,1)} %get-tuple-element.27, bf16[1,2048,1280]{1,2,0:T(8,128)(2,1)} %copy.9, f32[2048]{0:T(1024)S(1)} %multiply_multiply_fusion.1, f32[2048]{0:T(1024)S(1)} %copy-done.6), kind=kLoop, calls=%fused_computation.76 | loop fusion | flops 18350080 | bytes 20987904 | tf_op jit(solution)/shard_map/transpose(jvp())/add_any | solution.py:14
  546.4 29.8 %convolution_convert_fusion.3 = bf16[4352,1280]{1,0:T(8,128)(2,1)} fusion(bf16[2048,4352]{1,0:T(8,128)(2,1)} %get-tuple-element.20, bf16[2048,1280]{0,1:T(8,128)(2,1)} %fusion.66), kind=kOutput, calls=%fused_computation.25 | convolution fusion | flops 22822584320 | bytes 34209792 | tf_op jit(solution)/shard_map/transpose(jvp())/dot_general | solution.py:10
  576.2 0.0 reduce-scatter.15.cloned.1.call-update
  576.2 0.0 reduce-scatter.11.cloned.1.call-start
  576.3 50.0 %fusion.3 = (bf16[2048,4352]{1,0:T(8,128)(2,1)}, bf16[2048,4352]{1,0:T(8,128)(2,1)}) fusion(f32[2048,4352]{1,0:T(8,128)} %fusion.28, f32[2048,4352]{1,0:T(8,128)} %get-tuple-element.21, bf16[2048,1280]{0,1:T(8,128)(2,1)} %fusion.66, bf16[1,4352,1280]{2,1,0:T(8,128)(2,1)} %all-gather.17.cloned.1.call-done), kind=kOutput, calls=%fused_computation.9 | convolution fusion | flops 22932881408 | bytes 123338752 | tf_op jit(solution)/shard_map/transpose(jvp())/dot_general | solution.py:10
  626.3 37.4 %fusion.10 = bf16[1280,4352]{1,0:T(8,128)(2,1)} fusion(bf16[2048,4352]{1,0:T(8,128)(2,1)} %get-tuple-element.29, bf16[1,2048,1280]{1,2,0:T(8,128)(2,1)} %copy.10, f32[2048]{0:T(1024)S(1)} %copy-done.3, f32[2048,4352]{1,0:T(8,128)} %fusion.28), kind=kOutput, calls=%fused_computation.20 | convolution fusion | flops 22883926016 | bytes 69869568 | tf_op jit(solution)/shard_map/transpose(jvp())/dot_general | solution.py:22
  663.7 0.0 reduce-scatter.11.cloned.1.call-update
  663.7 0.0 reduce-scatter.13.cloned.1.call-start
  663.8 0.6 copy-done.7
  664.4 37.4 %fusion.11 = bf16[1280,4352]{1,0:T(8,128)(2,1)} fusion(bf16[2048,4352]{1,0:T(8,128)(2,1)} %convolution_convert_fusion.1, bf16[2048,1280]{0,1:T(8,128)(2,1)} %get-tuple-element.23, f32[2048]{0:T(1024)S(1)} %copy-done.7, f32[2048,4352]{1,0:T(8,128)} %get-tuple-element.25), kind=kOutput, calls=%fused_computation.21 | convolution fusion | flops 22883926016 | bytes 69869568 | tf_op jit(solution)/shard_map/transpose(jvp())/dot_general | solution.py:22
  701.8 0.0 reduce-scatter.9.cloned.1.call-start
  701.8 31.5 %convolution_convert_fusion.4 = bf16[1280,4352]{1,0:T(8,128)(2,1)} fusion(bf16[2048,4352]{1,0:T(8,128)(2,1)} %get-tuple-element.24, bf16[2048,1280]{0,1:T(8,128)(2,1)} %get-tuple-element.23, f32[2048]{0:T(1024)S(1)} %copy-done.7), kind=kOutput, calls=%fused_computation.26 | convolution fusion | flops 22824878080 | bytes 34217984 | tf_op jit(solution)/shard_map/transpose(jvp())/dot_general | solution.py:21
  733.4 0.0 reduce-scatter.9.cloned.1.call-update
  733.4 0.0 reduce-scatter.7.cloned.1.call-start
  733.5 31.1 %convolution_convert_fusion.5 = bf16[1280,4352]{1,0:T(8,128)(2,1)} fusion(bf16[2048,4352]{1,0:T(8,128)(2,1)} %get-tuple-element.28, bf16[1,2048,1280]{1,2,0:T(8,128)(2,1)} %copy.10, f32[2048]{0:T(1024)S(1)} %copy-done.3), kind=kOutput, calls=%fused_computation.27 | convolution fusion | flops 22824878080 | bytes 34217984 | tf_op jit(solution)/shard_map/transpose(jvp())/dot_general | solution.py:21
  764.6 0.0 reduce-scatter.7.cloned.1.call-update
  764.6 0.0 all-reduce.3.cloned.1.call-start
  764.6 33.7 %fusion.46 = bf16[2048,1280]{0,1:T(8,128)(2,1)} fusion(bf16[1,1280,4352]{2,1,0:T(8,128)(2,1)} %all-gather.15.cloned.1.call-done, bf16[2048,4352]{1,0:T(8,128)(2,1)} %get-tuple-element.29, f32[2048,4352]{1,0:T(8,128)} %fusion.28), kind=kOutput, calls=%fused_computation.68 | convolution fusion | flops 22873112576 | bytes 69861376 | tf_op jit(solution)/shard_map/transpose(jvp())/dot_general | solution.py:22
  798.3 78.0 %reduce-scatter.13.cloned.1.call-done = bf16[40,4352]{1,0:T(8,128)(2,1)} async-done(((bf16[1280,4352]{1,0:T(8,128)(2,1)}), bf16[40,4352]{1,0:T(8,128)(2,1)}) %reduce-scatter.13.cloned.1.call-update) | async-done | bytes 348176 | tf_op jit(solution)/shard_map/reduce_scatter | solution.py:31
  876.3 101.3 %reduce-scatter.9.cloned.1.call-done = bf16[40,4352]{1,0:T(8,128)(2,1)} async-done(((bf16[1280,4352]{1,0:T(8,128)(2,1)}), bf16[40,4352]{1,0:T(8,128)(2,1)}) %reduce-scatter.9.cloned.1.call-update) | async-done | bytes 348176 | tf_op jit(solution)/shard_map/reduce_scatter | solution.py:31
  977.6 101.1 %reduce-scatter.7.cloned.1.call-done = bf16[40,4352]{1,0:T(8,128)(2,1)} async-done(((bf16[1280,4352]{1,0:T(8,128)(2,1)}), bf16[40,4352]{1,0:T(8,128)(2,1)}) %reduce-scatter.7.cloned.1.call-update) | async-done | bytes 348176 | tf_op jit(solution)/shard_map/reduce_scatter | solution.py:31
  1078.7 0.0 all-reduce.3.cloned.1.call-update
  1078.8 33.1 %fusion.36 = (f32[2048]{0:T(1024)S(1)}, bf16[2048,1280]{0,1:T(8,128)(2,1)}) fusion(bf16[1,2048,1280]{1,2,0:T(8,128)(2,1)} %copy.10, bf16[2048,1280]{0,1:T(8,128)(2,1)} %fusion.46, bf16[2048,4352]{1,0:T(8,128)(2,1)} %get-tuple-element.28, bf16[1,1280,4352]{2,1,0:T(8,128)(2,1)} %all-gather.13.cloned.1.call-done), kind=kOutput, calls=%fused_computation.62 | convolution fusion | flops 22830118912 | bytes 44703744 | tf_op jit(solution)/shard_map/transpose(jvp())/dot_general | solution.py:21
  1111.9 12.4 %fusion.65 = bf16[1,2048,1280]{1,2,0:T(8,128)(2,1)} fusion(bf16[2048,1280]{0,1:T(8,128)(2,1)} %fusion.66, bf16[2048,1280]{0,1:T(8,128)(2,1)} %get-tuple-element.31, bf16[1,2048,1280]{1,2,0:T(8,128)(2,1)} %copy.10, f32[2048]{0:T(1024)S(1)} %multiply_multiply_fusion, f32[2048]{0:T(1024)S(1)} %copy-done.4), kind=kLoop, calls=%fused_computation.75 | loop fusion | flops 18350080 | bytes 20987904 | tf_op jit(solution)/shard_map/broadcast_in_dim | solution.py:44
  1124.3 7.9 copy.11
  1132.1 7.1 all-reduce.3.cloned.1.call-done
  1139.2 2.0 pad_maximum_fusion.2
  1141.2 2.5 pad_maximum_fusion
  (27 shorter events, 0.1 us)
Async XLA Ops:
  7.2 65.3 %all-gather.13.cloned.1.call-start = ((), (), s32[]{:S(2)}) async-start(), calls=%async_computation.12 | async-start | bytes 11489280 | tf_op jit(solution)/shard_map/all_gather | solution.py:28
  9.2 124.2 %all-gather.15.cloned.1.call-start = ((), (), s32[]{:S(2)}) async-start(), calls=%async_computation.13 | async-start | bytes 11489280 | tf_op jit(solution)/shard_map/all_gather | solution.py:28
  11.3 183.0 %all-gather.17.cloned.1.call-start = ((), (), s32[]{:S(2)}) async-start(), calls=%async_computation.14 | async-start | bytes 11489280 | tf_op jit(solution)/shard_map/all_gather | solution.py:28
  13.3 241.7 %all-gather.21.cloned.1.call-start = ((), (), s32[]{:S(2)}) async-start(), calls=%async_computation.16 | async-start | bytes 11489280 | tf_op jit(solution)/shard_map/all_gather | solution.py:28
  13.9 302.4 %all-gather.23.cloned.1.call-start = ((), (), s32[]{:S(2)}) async-start(), calls=%async_computation.17 | async-start | bytes 11489280 | tf_op jit(solution)/shard_map/all_gather | solution.py:28
  14.5 363.1 %all-gather.19.cloned.1.call-start = ((), (), s32[]{:S(2)}) async-start(), calls=%async_computation.15 | async-start | bytes 11489280 | tf_op jit(solution)/shard_map/all_gather | solution.py:28
  15.1 783.2 %reduce-scatter.17.cloned.1.call-start = ((), (), s32[]{:S(2)}) async-start(), calls=%async_computation.11 | async-start | bytes 11489280 | tf_op jit(solution)/shard_map/reduce_scatter | solution.py:31
  26.6 0.6 copy-start
  27.2 106.2 %copy-start.2 = (f32[2048]{0:T(1024)}, f32[2048]{0:T(1024)S(1)}, u32[]{:S(2)}) copy-start(f32[2048]{0:T(1024)S(1)} %fusion.77) | copy-start | bytes 24580
  226.3 59.2 %copy-start.8 = (f32[2048]{0:T(1024)}, f32[2048]{0:T(1024)S(1)}, u32[]{:S(2)}) copy-start(f32[2048]{0:T(1024)S(1)} %get-tuple-element.22) | copy-start | bytes 24580
  226.3 151.3 %copy-start.5 = (f32[2048]{0:T(1024)}, f32[2048]{0:T(1024)S(1)}, u32[]{:S(2)}) copy-start(f32[2048]{0:T(1024)S(1)} %fusion.78) | copy-start | bytes 24580
  467.2 331.1 %reduce-scatter.15.cloned.1.call-start = ((), (), s32[]{:S(2)}) async-start(), calls=%async_computation.10 | async-start | bytes 11489280 | tf_op jit(solution)/shard_map/reduce_scatter | solution.py:31
  501.0 33.1 %copy-start.9 = (f32[2048]{0:T(1024)S(1)}, f32[2048]{0:T(1024)}, u32[]{:S(2)}) copy-start(f32[2048]{0:T(1024)} %copy-done.8) | copy-start | bytes 24580
  501.0 33.1 %copy-start.6 = (f32[2048]{0:T(1024)S(1)}, f32[2048]{0:T(1024)}, u32[]{:S(2)}) copy-start(f32[2048]{0:T(1024)} %copy-done.5) | copy-start | bytes 24580
  576.2 222.1 %reduce-scatter.11.cloned.1.call-start = ((), (), s32[]{:S(2)}) async-start(), calls=%async_computation.8 | async-start | bytes 11489280 | tf_op jit(solution)/shard_map/reduce_scatter | solution.py:31
  576.2 50.0 %copy-start.3 = (f32[2048]{0:T(1024)S(1)}, f32[2048]{0:T(1024)}, u32[]{:S(2)}) copy-start(f32[2048]{0:T(1024)} %copy-done.2) | copy-start | bytes 24580
  663.7 0.7 copy-start.7
  663.7 212.6 %reduce-scatter.13.cloned.1.call-start = ((), (), s32[]{:S(2)}) async-start(), calls=%async_computation.9 | async-start | bytes 11489280 | tf_op jit(solution)/shard_map/reduce_scatter | solution.py:31
  701.8 275.8 %reduce-scatter.9.cloned.1.call-start = ((), (), s32[]{:S(2)}) async-start(), calls=%async_computation.7 | async-start | bytes 11489280 | tf_op jit(solution)/shard_map/reduce_scatter | solution.py:31
  733.4 345.3 %reduce-scatter.7.cloned.1.call-start = ((), (), s32[]{:S(2)}) async-start(), calls=%async_computation.6 | async-start | bytes 11489280 | tf_op jit(solution)/shard_map/reduce_scatter | solution.py:31
  764.6 374.6 %all-reduce.3.cloned.1.call-start = ((), (), s32[]{:S(2)}) async-start(), calls=%async_computation.18 | async-start | bytes 4177920 | tf_op jit(solution)/shard_map/psum | solution.py:31
  1078.7 33.1 %copy-start.1 = (f32[2048]{0:T(1024)S(1)}, f32[2048]{0:T(1024)}, u32[]{:S(2)}) copy-start(f32[2048]{0:T(1024)} %copy-done) | copy-start | bytes 24580
  1078.8 33.1 %copy-start.4 = (f32[2048]{0:T(1024)S(1)}, f32[2048]{0:T(1024)}, u32[]{:S(2)}) copy-start(f32[2048]{0:T(1024)} %copy-done.2) | copy-start | bytes 24580
Sparse Core Ops, SparseCore 0:
  10.9 61.5 all-gather.12
  74.8 58.5 all-gather.14
  135.7 58.5 all-gather.16
  196.4 58.5 all-gather.20
  257.8 58.5 all-gather.22
  319.1 58.5 all-gather.18
  467.3 97.5 reduce-scatter.16
  576.3 97.5 reduce-scatter.14
  677.8 97.3 reduce-scatter.10
  779.0 97.2 reduce-scatter.12
  880.2 97.3 reduce-scatter.8
  981.4 97.3 reduce-scatter.6
  1081.5 57.6 all-reduce.2
where the time goes:
time: 1160 us; the launch traced here: 1150 us
  matrix products  611 us (53%)
  waiting for transfers between devices  461 us (40%)
  other arithmetic  32.8 us (3%)
  local copies, waits for them, and re-layouts  30.9 us (3%)
  between operations  14.3 us (1%)
    reduce_scatter x6, waiting for transfers between devices, summed(): lax.psum_scatter(term, 's', scatter_dimension=0, tiled=True)  280 us
    dot_general x6, matrix products, layer(): up = jnp.dot(a, w['w_up'], preferred_element_type=jnp.float32)  218 us
    dot_general x6, matrix products, layer(): gate = jnp.dot(a, w['w_gate'], preferred_element_type=jnp.float32)  212 us
    dot_general x5, matrix products, matmul(): jnp.dot(a, w, preferred_element_type=jnp.float32).astype(jnp.bfloat16)  181 us
    all_gather x6, waiting for transfers between devices, fetched(): lax.all_gather(w[number], 's', axis=0, tiled=True)  172 us
    unnamed x23, local copies, waits for them, and re-layouts  24.9 us
  transfers between devices with their start and end apart: 13, of which 10 were waited for; matrix products, arithmetic and copies ran while one was open for 50% of the time, Pallas kernels for 0%

commit v1 on v0

v1 whole, which is shorter than its diff:
```python
import functools

import jax
import jax.numpy as jnp
from jax import lax
from jax.experimental import pallas as pl
from jax.experimental.pallas import tpu as pltpu
from jax.sharding import PartitionSpec as P

F32, BF16 = jnp.float32, jnp.bfloat16
SIDE = 4
VMEM_BYTES = 66 * 2**20 - 2**18


def matmul(a, w):
    return jnp.dot(a, w, preferred_element_type=F32).astype(BF16)


def dot_f32(a, w):
    return jnp.dot(a, w, preferred_element_type=F32)


def dot_nt(a, w):
    return lax.dot_general(a, w, (((1,), (1,)), ((), ())), preferred_element_type=F32).astype(BF16)


def dot_tn(a, w):
    return lax.dot_general(a, w, (((0,), (0,)), ((), ())), preferred_element_type=F32).astype(BF16)


def normed(h):
    wide = h.astype(F32)
    scale = lax.rsqrt(jnp.mean(wide**2, -1, keepdims=True) + 1e-6)
    return (wide * scale).astype(BF16)


def act(gate, up):
    return (jax.nn.silu(gate) * up).astype(BF16)


class Place:
    def __init__(self):
        self.s = lax.axis_index("s")
        self.r = lax.axis_index("r")
        self.k = self.s % 2
        self.y = self.s // (2 * SIDE)
        self.z = (self.s // 2) % SIDE
        self.b = self.y + self.k * (self.z - self.y)
        self.a = self.z + self.k * (self.y - self.z)

    def at(self, b, a):
        b, a = b % SIDE, a % SIDE
        y = b + self.k * (a - b)
        z = a + self.k * (b - a)
        return {"s": (y * SIDE + z) * 2 + self.k}

    def partner(self):
        return {"s": self.s + 1 - 2 * self.k}

    def group(self, bit):
        if bit == 1:
            return {"r": self.r + 1 - 2 * (self.r % 2)}
        return {"r": (self.r + 2) % 4}


MESH = pl.DeviceIdType.MESH


def send(src, dst, send_sem, recv_sem, to):
    return pltpu.make_async_remote_copy(src_ref=src, dst_ref=dst, send_sem=send_sem, recv_sem=recv_sem, device_id=to, device_id_type=MESH)


def meet(devices):
    barrier = pltpu.get_barrier_semaphore()
    for to in devices:
        pl.semaphore_signal(barrier, inc=1, device_id=to, device_id_type=MESH)
    pl.semaphore_wait(barrier, len(devices))


def wide(ref):
    return ref.astype(F32)


class Sum:
    def __init__(self, at, way, term, out, mine, theirs, rec, arec, xs, xr, sems):
        self.at, self.way, self.term, self.out = at, way, term, out
        self.mine, self.theirs, self.rec, self.arec, self.xs, self.xr = mine, theirs, rec, arec, xs, xr
        (self.local, self.pair_s, self.pair_r, self.b_s, self.b_r, self.a_s, self.a_r, self.x_s, self.x_r) = sems
        self.started = []

    def remote(self, *args):
        copy = send(*args)
        copy.start()
        self.started.append(copy)
        return copy

    def start(self):
        at = self.at
        self.loads = []
        self.pairs = []
        for j in range(SIDE):
            for core, (own, away) in enumerate(((self.term.at[j, :, 0], self.term.at[:, j, 1]), (self.term.at[:, j, 1], self.term.at[j, :, 0]))):
                load = pltpu.make_async_copy(own, self.mine.at[j], self.local.at[j])
                pair = send(away, self.theirs.at[j], self.pair_s.at[j], self.pair_r.at[j], at.partner())

                @pl.when(at.k == core)
                def _(load=load, pair=pair):
                    pair.start()
                    load.start()

                if core == 0:
                    self.loads.append(load)
                    self.pairs.append(pair)
        self.started += self.pairs

    def block(self, b, extra=()):
        @pl.loop(0, SIDE)
        def _(j):
            total = wide(self.mine[b, j]) + wide(self.theirs[b, j])
            for slot in extra:
                total = total + wide(self.rec[slot, j])
            self.theirs[b, j] = total.astype(BF16)

    def line(self, a):
        b = self.at.b
        return wide(self.mine[b, a]) + wide(self.theirs[b, a]) + wide(self.rec[1, a]) + wide(self.rec[2, a])

    def first(self):
        for load in self.loads:
            load.wait()
        for pair in self.pairs:
            pair.wait_recv()
        at, w = self.at, self.way
        far, back = (at.b + 2) % SIDE, (at.b - w) % SIDE
        self.block(far)
        self.far = self.remote(self.theirs.at[far], self.rec.at[0], self.b_s.at[0], self.b_r.at[0], at.at(at.b + w, at.a))
        self.block(back)
        self.back = self.remote(self.theirs.at[back], self.rec.at[2], self.b_s.at[2], self.b_r.at[2], at.at(at.b - w, at.a))

    def second(self):
        at, w = self.at, self.way
        near = (at.b + w) % SIDE
        self.far.wait_recv()
        self.block(near, (0,))
        self.near = self.remote(self.theirs.at[near], self.rec.at[1], self.b_s.at[1], self.b_r.at[1], at.at(at.b + w, at.a))

    def third(self):
        at, w = self.at, self.way
        self.back.wait_recv()
        self.near.wait_recv()
        far, back = (at.a + 2) % SIDE, (at.a - w) % SIDE
        self.theirs[at.b, far] = self.line(far).astype(BF16)
        self.far = self.remote(self.theirs.at[at.b, far], self.arec.at[0], self.a_s.at[0], self.a_r.at[0], at.at(at.b, at.a + w))
        self.theirs[at.b, back] = self.line(back).astype(BF16)
        self.back = self.remote(self.theirs.at[at.b, back], self.arec.at[2], self.a_s.at[2], self.a_r.at[2], at.at(at.b, at.a - w))

    def fourth(self):
        at, w = self.at, self.way
        near = (at.a + w) % SIDE
        self.far.wait_recv()
        self.theirs[at.b, near] = (self.line(near) + wide(self.arec[0])).astype(BF16)
        self.near = self.remote(self.theirs.at[at.b, near], self.arec.at[1], self.a_s.at[1], self.a_r.at[1], at.at(at.b, at.a + w))

    def fifth(self):
        at = self.at
        self.back.wait_recv()
        self.near.wait_recv()
        self.xs[0] = (self.line(at.a) + wide(self.arec[1]) + wide(self.arec[2])).astype(BF16)
        self.cross = self.remote(self.xs.at[0], self.xr.at[0], self.x_s.at[0], self.x_r.at[0], at.group(1))

    def sixth(self):
        self.cross.wait_recv()
        self.xs[1] = (wide(self.xs[0]) + wide(self.xr[0])).astype(BF16)
        self.cross = self.remote(self.xs.at[1], self.xr.at[1], self.x_s.at[1], self.x_r.at[1], self.at.group(2))

    def last(self):
        self.cross.wait_recv()
        self.out[...] = (wide(self.xs[1]) + wide(self.xr[1])).astype(BF16)

    def end(self):
        for copy in self.started:
            copy.wait_send()

    STAGES = ("start", "first", "second", "third", "fourth", "fifth", "sixth", "last", "end")


def sum_scratch(rows, columns):
    block, dma = (rows, columns), pltpu.SemaphoreType.DMA
    bufs = [pltpu.VMEM((SIDE, SIDE) + block, BF16)] * 2 + [pltpu.VMEM((3, SIDE) + block, BF16), pltpu.VMEM((3,) + block, BF16)]
    bufs += [pltpu.VMEM((2,) + block, BF16)] * 2
    return bufs + [dma((4,))] * 3 + [dma((3,))] * 4 + [dma((2,))] * 2


def summed(*terms, collective_id=1):
    shaped = [t.reshape(SIDE, SIDE, 2, t.shape[0] // 32, t.shape[1]) for t in terms]
    blocks = [t.shape[3:] for t in shaped]
    n = len(terms)

    def kernel(*refs):
        at = Place()
        ins, outs, scratch = refs[:n], refs[n : 2 * n], refs[2 * n :]
        sums = []
        for i in range(n):
            mine, theirs, rec, arec, xs, xr, *sems = scratch[15 * i : 15 * i + 15]
            sums.append(Sum(at, 1 if i % 2 == 0 else -1, ins[i], outs[i], mine, theirs, rec, arec, xs, xr, sems))
        meet([at.at(at.b + 1, at.a), at.at(at.b - 1, at.a), at.at(at.b, at.a + 1), at.at(at.b, at.a - 1), at.partner(), at.group(1), at.group(2)])
        for stage in Sum.STAGES:
            for one in sums:
                getattr(one, stage)()

    return pl.pallas_call(
        kernel,
        out_shape=[jax.ShapeDtypeStruct(block, BF16) for block in blocks],
        in_specs=[pl.BlockSpec(memory_space=pl.ANY)] * n,
        out_specs=[pl.BlockSpec(memory_space=pltpu.VMEM)] * n,
        scratch_shapes=[one for block in blocks for one in sum_scratch(*block)],
        compiler_params=pltpu.CompilerParams(collective_id=collective_id, has_side_effects=True, vmem_limit_bytes=VMEM_BYTES),
        name="summed",
    )(*shaped)


def solution(mesh):
    def fetched(w):
        return lax.all_gather(w, "s", axis=0, tiled=True)

    def scattered(term):
        return lax.psum(lax.psum_scatter(term, "s", scatter_dimension=0, tiled=True), "r")

    def step(x, dy, w_gate, w_up, w_down):
        x, dy = x[0], dy[0]
        gate0, up0, down0 = fetched(w_gate[0]), fetched(w_up[0]), fetched(w_down[0])
        gate1, up1, down1 = fetched(w_gate[1]), fetched(w_up[1]), fetched(w_down[1])

        a0, back_norm0 = jax.vjp(normed, x)
        g0, u0 = dot_f32(a0, gate0), dot_f32(a0, up0)
        m0, back_act0 = jax.vjp(act, g0, u0)
        h1 = x + matmul(m0, down0)
        a1, back_norm1 = jax.vjp(normed, h1)
        g1, u1 = dot_f32(a1, gate1), dot_f32(a1, up1)
        m1, back_act1 = jax.vjp(act, g1, u1)

        by_down1 = scattered(dot_tn(m1, dy))
        dg1, du1 = back_act1(dot_nt(dy, down1))
        dg1, du1 = dg1.astype(BF16), du1.astype(BF16)
        by_gate1 = scattered(dot_tn(a1, dg1))
        by_up1 = scattered(dot_tn(a1, du1))
        by_h1 = dy + back_norm1(dot_nt(dg1, gate1) + dot_nt(du1, up1))[0]

        t_down0 = dot_tn(m0, by_h1)
        dg0, du0 = back_act0(dot_nt(by_h1, down0))
        dg0, du0 = dg0.astype(BF16), du0.astype(BF16)
        t_gate0, t_up0 = dot_tn(a0, dg0), dot_tn(a0, du0)
        by_x = by_h1 + back_norm0(dot_nt(dg0, gate0) + dot_nt(du0, up0))[0]
        by_down0, by_gate0, by_up0 = summed(t_down0, t_gate0, t_up0)
        return by_x[None], jnp.stack([by_gate0, by_gate1]), jnp.stack([by_up0, by_up1]), jnp.stack([by_down0, by_down1])

    states, cut = P(("rep", "r", "s"), None, None), P(None, "s", None)
    return jax.shard_map(
        step,
        mesh=mesh,
        in_specs=(states, states) + (cut,) * 3,
        out_specs=(states,) + (P("rep", "s", None),) * 3,
        check_vma=False,
    )
```

time: 1160 us -> 1020 us (0.88)
  waiting for transfers between devices: 461 us -> 182 us
  Pallas kernels: 0 us -> 158 us
  matrix products: 611 us -> 592 us
    reduce_scatter x6 -> x3, waiting for transfers between devices: 280 us -> 0.06 us  [scattered(): lax.psum_scatter(term, 's', scatter_dimension=0, tiled=True)]
    pallas_call x0 -> x1, Pallas kernels: none -> 158 us  [summed(): pl.pallas_call(kernel, out_shape=[jax.ShapeDtypeStruct(block, BF16) for b...]
    dot_general x17, matrix products: 611 us -> 592 us  [the longest x6 205 us: dot_nt(): lax.dot_general(a, w, (((1,), (1,)), ((), ())), preferred_element_type=F32)]
    add_any x1 -> x0, other arithmetic: 12.3 us -> none  [normed(): wide = h.astype(jnp.float32)]
    add x0 -> x1, other arithmetic: none -> 12.3 us  [step(): by_h1 = dy + back_norm1(dot_nt(dg1, gate1) + dot_nt(du1, up1))[0]]
    unnamed x23 -> x25, local copies, waits for them, and re-layouts: 24.9 us -> 24.8 us
  transfers between devices with their start and end apart: 13 -> 10, of which waited for: 10 -> 6; matrix products, arithmetic and copies ran while one was open for 50% -> 55% of each run, Pallas kernels for 0% -> 16%
where the time goes in v1:
time: 1020 us; the launch traced here: 1010 us
  matrix products  592 us (58%)
  waiting for transfers between devices  182 us (18%)
  Pallas kernels  158 us (15%)
  other arithmetic  32.7 us (3%)
  local copies, waits for them, and re-layouts  30.7 us (3%)
  between operations  14.6 us (1%)
    dot_general x6, matrix products, dot_nt(): lax.dot_general(a, w, (((1,), (1,)), ((), ())), preferred_element_type=F32)  205 us
    dot_general x6, matrix products, dot_tn(): lax.dot_general(a, w, (((0,), (0,)), ((), ())), preferred_element_type=F32)  188 us
    all_gather x6, waiting for transfers between devices, fetched(): return lax.all_gather(w, 's', axis=0, tiled=True)  180 us
    dot_general x4, matrix products, dot_f32(): return jnp.dot(a, w, preferred_element_type=F32)  166 us
    pallas_call x1, Pallas kernels, summed(): pl.pallas_call(kernel, out_shape=[jax.ShapeDtypeStruct(block, BF16) for b...  158 us
    dot_general x1, matrix products, matmul(): return jnp.dot(a, w, preferred_element_type=F32).astype(BF16)  32 us
    unnamed x25, local copies, waits for them, and re-layouts  24.8 us
  transfers between devices with their start and end apart: 10, of which 6 were waited for; matrix products, arithmetic and copies ran while one was open for 55% of the time, Pallas kernels for 16%

profile of v1, /device:TPU:0, one launch (start us, length us, event | category | flops | bytes accessed | tf_op | source)
XLA Modules:
  0.0 1009.7 jit_solution(16556320163417429203)
XLA Ops:
  7.2 0.0 all-gather.15.cloned.1.call-start
  7.2 2.0 fusion.82
  9.2 0.0 all-gather.15.cloned.1.call-update
  9.2 0.0 all-gather.17.cloned.1.call-start
  9.3 2.0 fusion.81
  11.3 0.0 all-gather.17.cloned.1.call-update
  11.3 0.0 all-gather.19.cloned.1.call-start
  11.4 2.0 fusion.83
  13.4 0.0 all-gather.19.cloned.1.call-update
  13.4 0.0 all-gather.13.cloned.1.call-start
  13.4 0.5 all-gather.13.cloned.1.call-update
  14.0 0.0 all-gather.21.cloned.1.call-start
  14.0 0.5 all-gather.21.cloned.1.call-update
  14.5 0.0 all-gather.23.cloned.1.call-start
  14.6 0.5 all-gather.23.cloned.1.call-update
  15.1 0.0 reduce-scatter.8.cloned.1.call-start
  15.2 7.9 copy.10
  23.0 3.6 fusion.34
  26.6 0.6 copy-done.1
  27.2 45.3 %all-gather.15.cloned.1.call-done = bf16[1,1280,4352]{2,1,0:T(8,128)(2,1)} async-done(((bf16[1,40,4352]{2,1,0:T(8,128)(2,1)}), bf16[1,1280,4352]{2,1,0:T(8,128)(2,1)}) %all-gather.15.cloned.1.call-update) | async-done | bytes 11141136 | tf_op jit(solution)/shard_map/all_gather | solution.py:224
  72.5 32.1 %fusion.27 = f32[2048,4352]{1,0:T(8,128)} fusion(bf16[1,1280,4352]{2,1,0:T(8,128)(2,1)} %all-gather.15.cloned.1.call-done, bf16[1,2048,1280]{1,2,0:T(8,128)(2,1)} %copy.10, f32[2048]{0:T(1024)S(1)} %fusion.78), kind=kOutput, calls=%fused_computation.55 | convolution fusion | flops 22824878080 | bytes 52043776 | tf_op jit(solution)/shard_map/dot_general | solution.py:20
  104.6 28.8 %all-gather.17.cloned.1.call-done = bf16[1,1280,4352]{2,1,0:T(8,128)(2,1)} async-done(((bf16[1,40,4352]{2,1,0:T(8,128)(2,1)}), bf16[1,1280,4352]{2,1,0:T(8,128)(2,1)}) %all-gather.17.cloned.1.call-update) | async-done | bytes 11141136 | tf_op jit(solution)/shard_map/all_gather | solution.py:224
  133.4 43.4 %multiply_convert_fusion.1 = (bf16[2048,4352]{1,0:T(8,128)(2,1)}, f32[2048,4352]{1,0:T(8,128)}) fusion(f32[2048,4352]{1,0:T(8,128)} %fusion.27, bf16[1,1280,4352]{2,1,0:T(8,128)(2,1)} %all-gather.17.cloned.1.call-done, bf16[1,2048,1280]{1,2,0:T(8,128)(2,1)} %copy.10, f32[2048]{0:T(1024)S(1)} %fusion.78), kind=kOutput, calls=%fused_computation.17 | convolution fusion | flops 22878355456 | bytes 105521152 | tf_op jit(solution)/shard_map/dot_general | solution.py:20
  176.8 17.5 %all-gather.19.cloned.1.call-done = bf16[1,4352,1280]{2,1,0:T(8,128)(2,1)} async-done(((bf16[1,136,1280]{2,1,0:T(8,128)(2,1)}), bf16[1,4352,1280]{2,1,0:T(8,128)(2,1)}) %all-gather.19.cloned.1.call-update) | async-done | bytes 11141136 | tf_op jit(solution)/shard_map/all_gather | solution.py:224
  194.3 32.0 %fusion.37 = (f32[2048]{0:T(1024)S(1)}, bf16[2048,1280]{0,1:T(8,128)(2,1)}) fusion(bf16[2048,4352]{1,0:T(8,128)(2,1)} %get-tuple-element.27, bf16[1,4352,1280]{2,1,0:T(8,128)(2,1)} %all-gather.19.cloned.1.call-done, bf16[1,2048,1280]{1,2,0:T(8,128)(2,1)} %copy.10), kind=kOutput, calls=%fused_computation.65 | convolution fusion | flops 22830118912 | bytes 39460864 | tf_op jit(solution)/shard_map/dot_general | solution.py:16
  226.3 28.7 %all-gather.13.cloned.1.call-done = bf16[1,4352,1280]{2,1,0:T(8,128)(2,1)} async-done(((bf16[1,136,1280]{2,1,0:T(8,128)(2,1)}), bf16[1,4352,1280]{2,1,0:T(8,128)(2,1)}) %all-gather.13.cloned.1.call-update) | async-done | bytes 11141136 | tf_op jit(solution)/shard_map/all_gather | solution.py:224
  255.0 30.5 %convolution_convert_fusion.5 = bf16[2048,4352]{1,0:T(8,128)(2,1)} fusion(bf16[1,4352,1280]{2,1,0:T(8,128)(2,1)} %all-gather.13.cloned.1.call-done, bf16[1,2048,1280]{2,1,0:T(8,128)(2,1)} %param.6), kind=kOutput, calls=%fused_computation.25 | convolution fusion | flops 22825926656 | bytes 34209792 | tf_op jit(solution)/shard_map/dot_general | solution.py:24
  285.5 30.9 %all-gather.21.cloned.1.call-done = bf16[1,1280,4352]{2,1,0:T(8,128)(2,1)} async-done(((bf16[1,40,4352]{2,1,0:T(8,128)(2,1)}), bf16[1,1280,4352]{2,1,0:T(8,128)(2,1)}) %all-gather.21.cloned.1.call-update) | async-done | bytes 11141136 | tf_op jit(solution)/shard_map/all_gather | solution.py:224
  316.3 32.5 %fusion.16 = f32[2048,4352]{1,0:T(8,128)} fusion(bf16[1,1280,4352]{2,1,0:T(8,128)(2,1)} %all-gather.21.cloned.1.call-done, bf16[2048,1280]{0,1:T(8,128)(2,1)} %get-tuple-element.30, f32[2048]{0:T(1024)S(1)} %fusion.79), kind=kOutput, calls=%fused_computation.44 | convolution fusion | flops 22824878080 | bytes 52043776 | tf_op jit(solution)/shard_map/dot_general | solution.py:20
  348.8 28.8 %all-gather.23.cloned.1.call-done = bf16[1,1280,4352]{2,1,0:T(8,128)(2,1)} async-done(((bf16[1,40,4352]{2,1,0:T(8,128)(2,1)}), bf16[1,1280,4352]{2,1,0:T(8,128)(2,1)}) %all-gather.23.cloned.1.call-update) | async-done | bytes 11141136 | tf_op jit(solution)/shard_map/all_gather | solution.py:224
  377.6 58.1 %fusion.4 = (bf16[2048,4352]{1,0:T(8,128)(2,1)}, bf16[2048,4352]{1,0:T(8,128)(2,1)}, f32[2048,4352]{1,0:T(8,128)}) fusion(f32[2048,4352]{1,0:T(8,128)} %fusion.16, bf16[2048,4352]{1,0:T(8,128)(2,1)} %convolution_convert_fusion.5, bf16[1,1280,4352]{2,1,0:T(8,128)(2,1)} %all-gather.23.cloned.1.call-done, bf16[2048,1280]{0,1:T(8,128)(2,1)} %get-tuple-element.30, ...), kind=kOutput, calls=%fused_computation.10 | convolution fusion | flops 22958571520 | bytes 141172736 | tf_op jit(solution)/shard_map/dot_general | solution.py:20
  435.8 38.6 %convolution_convert_fusion.6 = bf16[4352,1280]{1,0:T(8,128)(2,1)} fusion(f32[2048,4352]{1,0:T(8,128)} %fusion.16, f32[2048,4352]{1,0:T(8,128)} %get-tuple-element.31, bf16[1,2048,1280]{2,1,0:T(8,128)(2,1)} %param.6), kind=kOutput, calls=%fused_computation.26 | convolution fusion | flops 22876061696 | bytes 87687168 | tf_op jit(solution)/shard_map/dot_general | solution.py:28
  474.4 0.0 reduce-scatter.8.cloned.1.call-update
  474.4 0.0 reduce-scatter.6.cloned.1.call-start
  474.4 31.4 %convolution_convert_fusion = bf16[1280,4352]{1,0:T(8,128)(2,1)} fusion(bf16[2048,4352]{1,0:T(8,128)(2,1)} %get-tuple-element.20, bf16[2048,1280]{0,1:T(8,128)(2,1)} %get-tuple-element.30, f32[2048]{0:T(1024)S(1)} %fusion.79), kind=kOutput, calls=%fused_computation.20 | convolution fusion | flops 22830448640 | bytes 34217984 | tf_op jit(solution)/shard_map/dot_general | solution.py:28
  505.8 0.0 reduce-scatter.6.cloned.1.call-update
  505.8 0.0 reduce-scatter.4.cloned.1.call-start
  505.9 0.0 slice-start.2
  505.9 8.4 copy.9
  514.3 29.6 %fusion.49 = bf16[2048,1280]{0,1:T(8,128)(2,1)S(1)} fusion(bf16[2048,4352]{1,0:T(8,128)(2,1)} %get-tuple-element.20, bf16[1,1280,4352]{2,1,0:T(8,128)(2,1)} %all-gather.21.cloned.1.call-done), kind=kOutput, calls=%fused_computation.71 | convolution fusion | flops 22819635200 | bytes 34209792 | tf_op jit(solution)/shard_map/dot_general | solution.py:24
  543.9 0.0 copy-start.6
  543.9 31.6 %fusion.39 = (f32[2048]{0:T(1024)S(1)}, bf16[2048,1280]{0,1:T(8,128)(2,1)}) fusion(bf16[2048,1280]{0,1:T(8,128)(2,1)S(1)} %bitcast.106, bf16[2048,1280]{0,1:T(8,128)(2,1)S(1)} %fusion.49, bf16[2048,4352]{1,0:T(8,128)(2,1)} %get-tuple-element.19, bf16[1,1280,4352]{2,1,0:T(8,128)(2,1)} %all-gather.23.cloned.1.call-done), kind=kOutput, calls=%fused_computation.67 | convolution fusion | flops 22832740352 | bytes 44703744 | tf_op jit(solution)/shard_map/dot_general | solution.py:24
  575.5 29.7 %convolution_convert_fusion.1 = bf16[1280,4352]{1,0:T(8,128)(2,1)} fusion(bf16[2048,4352]{1,0:T(8,128)(2,1)} %get-tuple-element.19, bf16[2048,1280]{0,1:T(8,128)(2,1)S(1)} %bitcast.106, f32[2048]{0:T(1024)S(1)} %fusion.79), kind=kOutput, calls=%fused_computation.21 | convolution fusion | flops 22830448640 | bytes 34217984 | tf_op jit(solution)/shard_map/dot_general | solution.py:28
  605.3 0.0 reduce-scatter.4.cloned.1.call-update
  605.3 0.0 all-reduce.3.cloned.1.call-start
  605.3 12.3 %fusion.67 = bf16[2048,1280]{0,1:T(8,128)(2,1)} fusion(bf16[2048,1280]{0,1:T(8,128)(2,1)} %get-tuple-element.30, bf16[2048,1280]{0,1:T(8,128)(2,1)} %get-tuple-element.33, bf16[1,2048,1280]{1,2,0:T(8,128)(2,1)} %copy.9, f32[2048]{0:T(1024)S(1)} %multiply_multiply_fusion.1, f32[2048]{0:T(1024)S(1)} %fusion.79), kind=kLoop, calls=%fused_computation.78 | loop fusion | flops 18350080 | bytes 20987904 | tf_op jit(solution)/shard_map/add | solution.py:247
  617.7 51.9 %fusion.1 = (bf16[2048,4352]{1,0:T(8,128)(2,1)}, bf16[2048,4352]{1,0:T(8,128)(2,1)}) fusion(f32[2048,4352]{1,0:T(8,128)} %fusion.27, f32[2048,4352]{1,0:T(8,128)} %get-tuple-element.28, bf16[2048,1280]{0,1:T(8,128)(2,1)} %fusion.67, bf16[1,4352,1280]{2,1,0:T(8,128)(2,1)} %all-gather.19.cloned.1.call-done), kind=kOutput, calls=%fused_computation.7 | convolution fusion | flops 22959620096 | bytes 123338752 | tf_op jit(solution)/shard_map/dot_general | solution.py:24
  669.5 29.6 %fusion.40 = bf16[2048,1280]{0,1:T(8,128)(2,1)S(1)} fusion(bf16[2048,4352]{1,0:T(8,128)(2,1)} %get-tuple-element.18, bf16[1,1280,4352]{2,1,0:T(8,128)(2,1)} %all-gather.15.cloned.1.call-done), kind=kOutput, calls=%fused_computation.68 | convolution fusion | flops 22819635200 | bytes 34209792 | tf_op jit(solution)/shard_map/dot_general | solution.py:24
  699.1 0.0 slice-start.1
  699.1 32.4 %fusion.36 = (f32[2048]{0:T(1024)S(1)}, bf16[2048,1280]{0,1:T(8,128)(2,1)}) fusion(bf16[1,2048,1280]{1,2,0:T(8,128)(2,1)} %copy.10, bf16[2048,1280]{0,1:T(8,128)(2,1)S(1)} %fusion.40, bf16[2048,4352]{1,0:T(8,128)(2,1)} %get-tuple-element.17, bf16[1,1280,4352]{2,1,0:T(8,128)(2,1)} %all-gather.17.cloned.1.call-done), kind=kOutput, calls=%fused_computation.64 | convolution fusion | flops 22832740352 | bytes 44703744 | tf_op jit(solution)/shard_map/dot_general | solution.py:24
  731.6 0.0 copy-start
  731.6 28.8 %convolution_convert_fusion.7 = bf16[4352,1280]{1,0:T(8,128)(2,1)} fusion(bf16[2048,4352]{1,0:T(8,128)(2,1)} %get-tuple-element.27, bf16[2048,1280]{0,1:T(8,128)(2,1)S(1)} %bitcast.101), kind=kOutput, calls=%fused_computation.27 | convolution fusion | flops 22822584320 | bytes 34209792 | tf_op jit(solution)/shard_map/dot_general | solution.py:28
  760.4 29.9 %convolution_convert_fusion.3 = bf16[1280,4352]{1,0:T(8,128)(2,1)} fusion(bf16[2048,4352]{1,0:T(8,128)(2,1)} %get-tuple-element.18, bf16[1,2048,1280]{1,2,0:T(8,128)(2,1)S(1)} %copy-done, f32[2048]{0:T(1024)S(1)} %copy-done.4), kind=kOutput, calls=%fused_computation.23 | convolution fusion | flops 22830448640 | bytes 34217984 | tf_op jit(solution)/shard_map/dot_general | solution.py:28
  790.3 29.8 %convolution_convert_fusion.2 = bf16[1280,4352]{1,0:T(8,128)(2,1)} fusion(bf16[2048,4352]{1,0:T(8,128)(2,1)} %get-tuple-element.17, bf16[1,2048,1280]{1,2,0:T(8,128)(2,1)S(1)} %copy-done, f32[2048]{0:T(1024)S(1)} %copy-done.4), kind=kOutput, calls=%fused_computation.22 | convolution fusion | flops 22830448640 | bytes 34217984 | tf_op jit(solution)/shard_map/dot_general | solution.py:28
  820.1 0.0 reduce-scatter.8.cloned.1.call-done
  820.1 0.0 reduce-scatter.6.cloned.1.call-done
  820.2 0.0 reduce-scatter.4.cloned.1.call-done
  820.2 0.0 all-reduce.3.cloned.1.call-update
  820.2 12.3 %fusion.66 = bf16[1,2048,1280]{1,2,0:T(8,128)(2,1)} fusion(bf16[2048,1280]{0,1:T(8,128)(2,1)} %fusion.67, bf16[2048,1280]{0,1:T(8,128)(2,1)} %get-tuple-element.35, bf16[1,2048,1280]{1,2,0:T(8,128)(2,1)} %copy.10, f32[2048]{0:T(1024)S(1)} %multiply_multiply_fusion, f32[2048]{0:T(1024)S(1)} %copy-done.4), kind=kLoop, calls=%fused_computation.77 | loop fusion | flops 18350080 | bytes 20987904 | tf_op jit(solution)/shard_map/broadcast_in_dim | solution.py:255
  832.5 7.9 copy.11
  840.4 157.7 %summed.1 = (bf16[136,1280]{1,0:T(8,128)(2,1)}, bf16[40,4352]{1,0:T(8,128)(2,1)}, bf16[40,4352]{1,0:T(8,128)(2,1)}) custom-call(bf16[4,4,2,136,1280]{4,3,2,1,0:T(8,128)(2,1)} %bitcast.102, bf16[4,4,2,40,4352]{4,3,2,1,0:T(8,128)(2,1)} %bitcast.103, bf16[4,4,2,40,4352]{4,3,2,1,0:T(8,128)(2,1)} %bitcast.104), custom_call_target="tpu_custom_call" | custom-call | tf_op jit(solution)/shard_map/summed/pallas_call | solution.py:211
  998.1 0.0 all-reduce.3.cloned.1.call-done
  998.1 2.0 pad_maximum_fusion.2
  1000.1 2.5 pad_maximum_fusion
  (23 shorter events, 0.1 us)
Async XLA Ops:
  7.2 65.3 %all-gather.15.cloned.1.call-start = ((), (), s32[]{:S(2)}) async-start(), calls=%async_computation.7 | async-start | bytes 11489280 | tf_op jit(solution)/shard_map/all_gather | solution.py:224
  9.2 124.2 %all-gather.17.cloned.1.call-start = ((), (), s32[]{:S(2)}) async-start(), calls=%async_computation.8 | async-start | bytes 11489280 | tf_op jit(solution)/shard_map/all_gather | solution.py:224
  11.3 183.0 %all-gather.19.cloned.1.call-start = ((), (), s32[]{:S(2)}) async-start(), calls=%async_computation.9 | async-start | bytes 11489280 | tf_op jit(solution)/shard_map/all_gather | solution.py:224
  13.4 241.6 %all-gather.13.cloned.1.call-start = ((), (), s32[]{:S(2)}) async-start(), calls=%async_computation.6 | async-start | bytes 11489280 | tf_op jit(solution)/shard_map/all_gather | solution.py:224
  14.0 302.4 %all-gather.21.cloned.1.call-start = ((), (), s32[]{:S(2)}) async-start(), calls=%async_computation.10 | async-start | bytes 11489280 | tf_op jit(solution)/shard_map/all_gather | solution.py:224
  14.5 363.1 %all-gather.23.cloned.1.call-start = ((), (), s32[]{:S(2)}) async-start(), calls=%async_computation.11 | async-start | bytes 11489280 | tf_op jit(solution)/shard_map/all_gather | solution.py:224
  15.1 805.0 %reduce-scatter.8.cloned.1.call-start = ((), (), s32[]{:S(2)}) async-start(), calls=%async_computation.5 | async-start | bytes 11489280 | tf_op jit(solution)/shard_map/reduce_scatter | solution.py:227
  26.6 0.6 copy-start.1
  27.2 106.1 %copy-start.3 = (f32[2048]{0:T(1024)}, f32[2048]{0:T(1024)S(1)}, u32[]{:S(2)}) copy-start(f32[2048]{0:T(1024)S(1)} %fusion.78) | copy-start | bytes 24580
  226.3 59.2 %copy-start.5 = (f32[2048]{0:T(1024)}, f32[2048]{0:T(1024)S(1)}, u32[]{:S(2)}) copy-start(f32[2048]{0:T(1024)S(1)} %get-tuple-element.29) | copy-start | bytes 24580
  474.4 345.8 %reduce-scatter.6.cloned.1.call-start = ((), (), s32[]{:S(2)}) async-start(), calls=%async_computation.4 | async-start | bytes 11489280 | tf_op jit(solution)/shard_map/reduce_scatter | solution.py:227
  505.8 314.3 %reduce-scatter.4.cloned.1.call-start = ((), (), s32[]{:S(2)}) async-start(), calls=%async_computation.3 | async-start | bytes 11489280 | tf_op jit(solution)/shard_map/reduce_scatter | solution.py:227
  505.9 38.0 %slice-start.2 = ((s8[5242880]{0:T(1024)(128)(4,1)}), s8[1048576]{0:T(1024)(128)(4,1)S(1)}, s32[]{:S(2)}) async-start(s8[5242880]{0:T(1024)(128)(4,1)} %bitcast.105), calls=%async_computation.15 | async-start | bytes 2097152
  514.3 29.6 %slice-start.3 = ((s8[5242880]{0:T(1024)(128)(4,1)}), s8[4194304]{0:T(1024)(128)(4,1)S(1)}, s32[]{:S(2)}) async-start(s8[5242880]{0:T(1024)(128)(4,1)} %bitcast.105), calls=%async_computation.16 | async-start | bytes 8388608
  543.9 31.6 %copy-start.6 = (f32[2048]{0:T(1024)S(1)}, f32[2048]{0:T(1024)}, u32[]{:S(2)}) copy-start(f32[2048]{0:T(1024)} %copy-done.5) | copy-start | bytes 24580
  605.3 392.8 %all-reduce.3.cloned.1.call-start = ((), (), s32[]{:S(2)}) async-start(), calls=%async_computation.12 | async-start | bytes 2088960 | tf_op jit(solution)/shard_map/psum | solution.py:227
  669.5 62.0 %slice-start = ((s8[5242880]{0:T(1024)(128)(4,1)}), s8[4194304]{0:T(1024)(128)(4,1)S(1)}, s32[]{:S(2)}) async-start(s8[5242880]{0:T(1024)(128)(4,1)} %bitcast.100), calls=%async_computation.13 | async-start | bytes 8388608
  699.1 32.4 %copy-start.2 = (f32[2048]{0:T(1024)S(1)}, f32[2048]{0:T(1024)}, u32[]{:S(2)}) copy-start(f32[2048]{0:T(1024)} %copy-done.1) | copy-start | bytes 24580
  699.1 32.4 %slice-start.1 = ((s8[5242880]{0:T(1024)(128)(4,1)}), s8[1048576]{0:T(1024)(128)(4,1)S(1)}, s32[]{:S(2)}) async-start(s8[5242880]{0:T(1024)(128)(4,1)} %bitcast.100), calls=%async_computation.14 | async-start | bytes 2097152
  731.6 28.8 %copy-start = (bf16[1,2048,1280]{1,2,0:T(8,128)(2,1)S(1)}, bf16[1,2048,1280]{1,2,0:T(8,128)(2,1)}, u32[]{:S(2)}) copy-start(bf16[1,2048,1280]{1,2,0:T(8,128)(2,1)} %copy.10) | copy-start | bytes 15728644
  731.6 28.8 %copy-start.4 = (f32[2048]{0:T(1024)S(1)}, f32[2048]{0:T(1024)}, u32[]{:S(2)}) copy-start(f32[2048]{0:T(1024)} %copy-done.3) | copy-start | bytes 24580
Sparse Core Ops, SparseCore 0:
  10.9 61.5 all-gather.14
  74.8 58.5 all-gather.16
  135.7 58.5 all-gather.18
  196.5 58.5 all-gather.12
  257.8 58.5 all-gather.20
  319.1 58.5 all-gather.22
  474.5 97.6 reduce-scatter.7
  576.1 97.3 reduce-scatter.5
  677.4 97.3 reduce-scatter.3
  820.3 45.2 all-reduce.2

commit v2 on v1

v2 whole, which is shorter than its diff:
```python
import functools

import jax
import jax.numpy as jnp
from jax import lax
from jax.experimental import pallas as pl
from jax.experimental.pallas import tpu as pltpu
from jax.sharding import PartitionSpec as P

F32, BF16 = jnp.float32, jnp.bfloat16
SIDE = 4
VMEM_BYTES = 66 * 2**20 - 2**18


def matmul(a, w):
    return jnp.dot(a, w, preferred_element_type=F32).astype(BF16)


def dot_f32(a, w):
    return jnp.dot(a, w, preferred_element_type=F32)


def dot_nt(a, w):
    return lax.dot_general(a, w, (((1,), (1,)), ((), ())), preferred_element_type=F32).astype(BF16)


def dot_tn(a, w):
    return lax.dot_general(a, w, (((0,), (0,)), ((), ())), preferred_element_type=F32).astype(BF16)


def normed(h):
    wide = h.astype(F32)
    scale = lax.rsqrt(jnp.mean(wide**2, -1, keepdims=True) + 1e-6)
    return (wide * scale).astype(BF16)


def act(gate, up):
    return (jax.nn.silu(gate) * up).astype(BF16)


class Place:
    def __init__(self):
        self.s = lax.axis_index("s")
        self.r = lax.axis_index("r")
        self.k = self.s % 2
        self.y = self.s // (2 * SIDE)
        self.z = (self.s // 2) % SIDE
        self.b = self.y + self.k * (self.z - self.y)
        self.a = self.z + self.k * (self.y - self.z)

    def at(self, b, a):
        b, a = b % SIDE, a % SIDE
        y = b + self.k * (a - b)
        z = a + self.k * (b - a)
        return {"s": (y * SIDE + z) * 2 + self.k}

    def partner(self):
        return {"s": self.s + 1 - 2 * self.k}

    def group(self, bit):
        if bit == 1:
            return {"r": self.r + 1 - 2 * (self.r % 2)}
        return {"r": (self.r + 2) % 4}


MESH = pl.DeviceIdType.MESH


def send(src, dst, send_sem, recv_sem, to):
    return pltpu.make_async_remote_copy(src_ref=src, dst_ref=dst, send_sem=send_sem, recv_sem=recv_sem, device_id=to, device_id_type=MESH)


def meet(devices):
    barrier = pltpu.get_barrier_semaphore()
    for to in devices:
        pl.semaphore_signal(barrier, inc=1, device_id=to, device_id_type=MESH)
    pl.semaphore_wait(barrier, len(devices))


def wide(ref):
    return ref.astype(F32)


class Sum:
    STAGES = ("start", "first", "second", "third", "fourth", "fifth", "sixth", "last", "end")

    def __init__(self, at, way, term, out, mine, theirs, rec, arec, xs, xr, local, pair_s, pair_r, b_s, b_r, a_s, a_r, x_s, x_r):
        self.at, self.out = at, out
        self.mine, self.theirs, self.rec, self.arec, self.xs, self.xr = mine, theirs, rec, arec, xs, xr
        b, a = at.b, at.a
        self.b_far, self.b_near, self.b_back = (b + 2) % SIDE, (b + way) % SIDE, (b - way) % SIDE
        self.a_far, self.a_near, self.a_back = (a + 2) % SIDE, (a + way) % SIDE, (a - way) % SIDE
        self.loads, self.pairs = [[], []], [[], []]
        for j in range(SIDE):
            for core, (own, away) in enumerate(((term.at[j, :, 0], term.at[:, j, 1]), (term.at[:, j, 1], term.at[j, :, 0]))):
                self.loads[core].append(pltpu.make_async_copy(own, mine.at[j], local.at[j]))
                self.pairs[core].append(send(away, theirs.at[j], pair_s.at[j], pair_r.at[j], at.partner()))
        ahead, behind = at.at(b + way, a), at.at(b - way, a)
        self.far = send(theirs.at[self.b_far], rec.at[0], b_s.at[0], b_r.at[0], ahead)
        self.near = send(theirs.at[self.b_near], rec.at[1], b_s.at[1], b_r.at[1], ahead)
        self.back = send(theirs.at[self.b_back], rec.at[2], b_s.at[2], b_r.at[2], behind)
        ahead, behind = at.at(b, a + way), at.at(b, a - way)
        self.far2 = send(theirs.at[b, self.a_far], arec.at[0], a_s.at[0], a_r.at[0], ahead)
        self.near2 = send(theirs.at[b, self.a_near], arec.at[1], a_s.at[1], a_r.at[1], ahead)
        self.back2 = send(theirs.at[b, self.a_back], arec.at[2], a_s.at[2], a_r.at[2], behind)
        self.cross = [send(xs.at[i], xr.at[i], x_s.at[i], x_r.at[i], at.group(i + 1)) for i in range(2)]

    def block(self, b, extra=()):
        @pl.loop(0, SIDE)
        def _(j):
            total = wide(self.mine[b, j]) + wide(self.theirs[b, j])
            for slot in extra:
                total = total + wide(self.rec[slot, j])
            self.theirs[b, j] = total.astype(BF16)

    def line(self, a):
        b = self.at.b
        return wide(self.mine[b, a]) + wide(self.theirs[b, a]) + wide(self.rec[1, a]) + wide(self.rec[2, a])

    def start(self):
        for core in range(2):

            @pl.when(self.at.k == core)
            def _():
                for pair, load in zip(self.pairs[core], self.loads[core]):
                    pair.start()
                    load.start()

    def first(self):
        for pair, load in zip(self.pairs[0], self.loads[0]):
            load.wait()
            pair.wait_recv()
        self.block(self.b_far)
        self.far.start()
        self.block(self.b_back)
        self.back.start()

    def second(self):
        self.far.wait_recv()
        self.block(self.b_near, (0,))
        self.near.start()

    def third(self):
        self.back.wait_recv()
        self.near.wait_recv()
        b = self.at.b
        self.theirs[b, self.a_far] = self.line(self.a_far).astype(BF16)
        self.far2.start()
        self.theirs[b, self.a_back] = self.line(self.a_back).astype(BF16)
        self.back2.start()

    def fourth(self):
        self.far2.wait_recv()
        self.theirs[self.at.b, self.a_near] = (self.line(self.a_near) + wide(self.arec[0])).astype(BF16)
        self.near2.start()

    def fifth(self):
        self.back2.wait_recv()
        self.near2.wait_recv()
        self.xs[0] = (self.line(self.at.a) + wide(self.arec[1]) + wide(self.arec[2])).astype(BF16)
        self.cross[0].start()

    def sixth(self):
        self.cross[0].wait_recv()
        self.xs[1] = (wide(self.xs[0]) + wide(self.xr[0])).astype(BF16)
        self.cross[1].start()

    def last(self):
        self.cross[1].wait_recv()
        self.out[...] = (wide(self.xs[1]) + wide(self.xr[1])).astype(BF16)

    def end(self):
        for copy in self.pairs[0] + [self.far, self.near, self.back, self.far2, self.near2, self.back2] + self.cross:
            copy.wait_send()


class Gather:
    STAGES = ("start", "first", "second", "third", "fourth", "end")

    def __init__(self, at, block, whole, own_s, a_s, a_r, b_s, b_r, p_s, p_r):
        b, a, half = at.b, at.a, block.shape[1] // 2

        def spot(db, da):
            row, column = (b + db) % SIDE, (a + da) % SIDE
            return whole.at[row + at.k * (column - row), column + at.k * (row - column), at.k]

        right, left = at.at(b, a + 1), at.at(b, a - 1)
        up, down = at.at(b + 1, a), at.at(b - 1, a)
        self.own = pltpu.make_async_copy(block, spot(0, 0), own_s)
        self.along = [send(block, spot(0, 0), a_s.at[0], a_r.at[0], right), send(block, spot(0, 0), a_s.at[1], a_r.at[1], left)]
        sides = (pl.ds(0, half), pl.ds(half, half))
        self.along += [
            send(spot(0, da).at[:, side], spot(0, da).at[:, side], a_s.at[2 + i], a_r.at[2 + i], to)
            for i, (da, side, to) in enumerate(((-1, sides[0], right), (1, sides[1], left)))
        ]
        steps = (0, -1, 1, 2)
        self.to_up = [send(block if i == 0 else spot(0, da), spot(0, da), b_s.at[i], b_r.at[i], up) for i, da in enumerate(steps)]
        self.to_down = [send(block if i == 0 else spot(0, da), spot(0, da), b_s.at[4 + i], b_r.at[4 + i], down) for i, da in enumerate(steps)]
        self.far = [
            send(spot(-1 if i < 2 else 1, da), spot(-1 if i < 2 else 1, da), b_s.at[8 + i], b_r.at[8 + i], up if i < 2 else down) for i, da in enumerate(steps)
        ]
        self.pair = [
            send(block if i == 0 and db == 0 else spot(db, da), spot(db, da), p_s.at[4 * j + i], p_r.at[4 * j + i], at.partner())
            for j, db in enumerate((0, -1, 1, 2))
            for i, da in enumerate(steps)
        ]

    def start(self):
        for copy in (self.along[0], self.along[1], self.to_up[0], self.to_down[0], self.pair[0], self.own):
            copy.start()

    def first(self):
        for i in (0, 1):
            self.along[i].wait_recv()
            for copy in (self.along[2 + i], self.to_up[1 + i], self.to_down[1 + i], self.pair[1 + i]):
                copy.start()

    def second(self):
        self.along[2].wait_recv()
        self.along[3].wait_recv()
        for copy in (self.to_up[3], self.to_down[3], self.pair[3]):
            copy.start()

    def third(self):
        for i in range(4):
            for j, arrived in ((4, self.to_up), (8, self.to_down)):
                arrived[i].wait_recv()
                if (i < 2) == (j == 4):
                    self.far[i].start()
                self.pair[j + i].start()

    def fourth(self):
        for i in range(4):
            self.far[i].wait_recv()
            self.pair[12 + i].start()

    def end(self):
        for copy in self.pair:
            copy.wait_recv()
        for copy in self.along + self.to_up + self.to_down + self.far + self.pair:
            copy.wait_send()
        self.own.wait()


DMA = pltpu.SemaphoreType.DMA
GATHER_SCRATCH = 7
SUM_SCRATCH = 15


def gather_scratch():
    return [DMA, DMA((4,)), DMA((4,)), DMA((12,)), DMA((12,)), DMA((16,)), DMA((16,))]


def sum_scratch(rows, columns):
    block = (rows, columns)
    bufs = [pltpu.VMEM((SIDE, SIDE) + block, BF16)] * 2 + [pltpu.VMEM((3, SIDE) + block, BF16), pltpu.VMEM((3,) + block, BF16)]
    bufs += [pltpu.VMEM((2,) + block, BF16)] * 2
    return bufs + [DMA((4,))] * 3 + [DMA((3,))] * 4 + [DMA((2,))] * 2


def neighbours(at, groups):
    near = [at.at(at.b + 1, at.a), at.at(at.b - 1, at.a), at.at(at.b, at.a + 1), at.at(at.b, at.a - 1), at.partner()]
    return near + ([at.group(1), at.group(2)] if groups else [])


def params(collective_id, has_side_effects=True):
    return pltpu.CompilerParams(collective_id=collective_id, has_side_effects=has_side_effects, vmem_limit_bytes=VMEM_BYTES)


def local_params():
    return pltpu.CompilerParams(vmem_limit_bytes=VMEM_BYTES)


def cost(matmuls, mebibytes):
    return pl.CostEstimate(flops=matmuls * 2 * 2048 * 1280 * 4352, bytes_accessed=mebibytes * 2**20, transcendentals=0)


ANY = pl.BlockSpec(memory_space=pl.ANY)
WHOLE = pl.BlockSpec(memory_space=pltpu.VMEM)


def in_turn(tasks):
    for stage in tasks[0].STAGES:
        for task in tasks:
            getattr(task, stage)()


def beside(tasks, steps):
    now = pl.program_id(0)
    for step in sorted(set(sum(map(list, steps), []))):

        @pl.when(now == step)
        def _():
            for stage in range(len(tasks[0].STAGES)):
                for task, when in zip(tasks, steps):
                    if when[stage] == step:
                        getattr(task, task.STAGES[stage])()


def shaped_term(t):
    return t.reshape(SIDE, SIDE, 2, t.shape[0] // 32, t.shape[1])


def whole_shape(block):
    return jax.ShapeDtypeStruct((SIDE, SIDE, 2) + block.shape, BF16)


def flat(whole):
    return whole.reshape(-1, whole.shape[-1])


def gathered(*blocks, collective_id):
    n = len(blocks)

    def kernel(*refs):
        at = Place()
        tasks = [Gather(at, refs[i], refs[n + i], *refs[2 * n + GATHER_SCRATCH * i : 2 * n + GATHER_SCRATCH * (i + 1)]) for i in range(n)]
        meet(neighbours(at, False))
        in_turn(tasks)

    outs = pl.pallas_call(
        kernel,
        out_shape=[whole_shape(b) for b in blocks],
        in_specs=[WHOLE] * n,
        out_specs=[ANY] * n,
        scratch_shapes=gather_scratch() * n,
        compiler_params=params(collective_id),
        cost_estimate=cost(3, 30),
        name="gathered",
    )(*blocks)
    return [flat(o) for o in outs]


def sums_of(at, n, ins, outs, scratch):
    return [Sum(at, 1 if i % 2 == 0 else -1, ins[i], outs[i], *scratch[SUM_SCRATCH * i : SUM_SCRATCH * (i + 1)]) for i in range(n)]


def summed(*terms, collective_id):
    shaped = [shaped_term(t) for t in terms]
    n = len(terms)

    def kernel(*refs):
        at = Place()
        tasks = sums_of(at, n, refs[:n], refs[n : 2 * n], refs[2 * n :])
        meet(neighbours(at, True))
        in_turn(tasks)

    return pl.pallas_call(
        kernel,
        out_shape=[jax.ShapeDtypeStruct(t.shape[3:], BF16) for t in shaped],
        in_specs=[ANY] * n,
        out_specs=[WHOLE] * n,
        scratch_shapes=[one for t in shaped for one in sum_scratch(*t.shape[3:])],
        compiler_params=params(collective_id),
        cost_estimate=cost(4, 60),
        name="summed",
    )(*shaped)


TILE = 256
ROWS = 512


def dot_nt_f32(a, w):
    return lax.dot_general(a, w, (((1,), (1,)), ((), ())), preferred_element_type=F32)


def act_body(g, u):
    return (g * jax.nn.sigmoid(g) * u).astype(BF16)


def act_back(g, u, dm):
    s = jax.nn.sigmoid(g)
    silu = g * s
    return (dm * u * (s + silu * (1.0 - s))).astype(BF16), (dm * silu).astype(BF16)


def whole_block(shape):
    return pl.BlockSpec(shape, lambda j: (0, 0))


def column_block(rows):
    return pl.BlockSpec((rows, TILE), lambda j: (0, j))


def row_block(columns):
    return pl.BlockSpec((TILE, columns), lambda j: (j, 0))


def gate_up(a, gate, up, blocks, collective_id):
    tokens, d = a.shape
    hidden, n = gate.shape[1], len(blocks)
    last = hidden // TILE - 1

    def kernel(a_ref, gate_ref, up_ref, *refs):
        ins, (g_ref, u_ref, m_ref), outs, scratch = refs[:n], refs[n : n + 3], refs[n + 3 : 2 * n + 3], refs[2 * n + 3 :]
        at = Place()
        tasks = [Gather(at, ins[i], outs[i], *scratch[GATHER_SCRATCH * i : GATHER_SCRATCH * (i + 1)]) for i in range(n)]

        @pl.when(pl.program_id(0) == 0)
        def _():
            meet(neighbours(at, False))

        beside(tasks, [GATHER_STEPS] * n)
        for i in range(tokens // ROWS):
            r = pl.ds(i * ROWS, ROWS)
            g, u = dot_f32(a_ref[r], gate_ref[...]), dot_f32(a_ref[r], up_ref[...])
            g_ref[r], u_ref[r], m_ref[r] = g, u, act_body(g, u)

    GATHER_STEPS = (0, 4, 7, 12, 15, last)
    outs = pl.pallas_call(
        kernel,
        grid=(last + 1,),
        out_shape=[jax.ShapeDtypeStruct((tokens, hidden), t) for t in (F32, F32, BF16)] + [whole_shape(b) for b in blocks],
        in_specs=[whole_block((tokens, d)), column_block(d), column_block(d)] + [WHOLE] * n,
        out_specs=[column_block(tokens)] * 3 + [ANY] * n,
        scratch_shapes=gather_scratch() * n,
        compiler_params=params(collective_id),
        cost_estimate=cost(2, 110),
        name="gate_up",
    )(a, gate, up, *blocks)
    return outs[:3], [flat(o) for o in outs[3:]]


def middle(a, dy, gate, up, down):
    tokens, d = a.shape
    hidden = gate.shape[1]

    def kernel(a_ref, dy_ref, gate_ref, up_ref, down_ref, m_ref, dg_ref, du_ref):
        for i in range(tokens // ROWS):
            r = pl.ds(i * ROWS, ROWS)
            g, u = dot_f32(a_ref[r], gate_ref[...]), dot_f32(a_ref[r], up_ref[...])
            dm = wide(dot_nt_f32(dy_ref[r], down_ref[...]).astype(BF16))
            m_ref[r] = act_body(g, u)
            dg_ref[r], du_ref[r] = act_back(g, u, dm)

    return pl.pallas_call(
        kernel,
        grid=(hidden // TILE,),
        out_shape=[jax.ShapeDtypeStruct((tokens, hidden), BF16)] * 3,
        in_specs=[whole_block((tokens, d))] * 2 + [column_block(d)] * 2 + [row_block(d)],
        out_specs=[column_block(tokens)] * 3,
        compiler_params=local_params(),
        cost_estimate=cost(3, 100),
        name="middle",
    )(a, dy, gate, up, down)


def back_down(dy, down, g, u, terms, collective_id):
    tokens, d = dy.shape
    hidden, n = down.shape[0], len(terms)
    shaped = [shaped_term(t) for t in terms]
    last = hidden // TILE - 1
    steps = (0, 4, 8, 13, 15, last, last, last, last)

    def kernel(dy_ref, down_ref, g_ref, u_ref, *refs):
        ins, (dg_ref, du_ref), outs, scratch = refs[:n], refs[n : n + 2], refs[n + 2 : 2 * n + 2], refs[2 * n + 2 :]
        at = Place()
        tasks = sums_of(at, n, ins, outs, scratch)

        @pl.when(pl.program_id(0) == 0)
        def _():
            meet(neighbours(at, True))

        beside(tasks, [steps] * n)
        for i in range(tokens // ROWS):
            r = pl.ds(i * ROWS, ROWS)
            dm = wide(dot_nt_f32(dy_ref[r], down_ref[...]).astype(BF16))
            dg_ref[r], du_ref[r] = act_back(g_ref[r], u_ref[r], dm)

    outs = pl.pallas_call(
        kernel,
        grid=(last + 1,),
        out_shape=[jax.ShapeDtypeStruct((tokens, hidden), BF16)] * 2 + [jax.ShapeDtypeStruct(t.shape[3:], BF16) for t in shaped],
        in_specs=[whole_block((tokens, d)), row_block(d), column_block(tokens), column_block(tokens)] + [ANY] * n,
        out_specs=[column_block(tokens)] * 2 + [WHOLE] * n,
        scratch_shapes=[one for t in shaped for one in sum_scratch(*t.shape[3:])],
        compiler_params=params(collective_id),
        cost_estimate=cost(2, 120),
        name="back_down",
    )(dy, down, g, u, *shaped)
    return outs[:2], outs[2:]


def back_up(dg, du, gate, up, terms, collective_id):
    tokens, hidden = dg.shape
    d, n = gate.shape[0], len(terms)
    shaped = [shaped_term(t) for t in terms]
    last = hidden // TILE - 1
    steps = ((0, 4, 9, 14, last, last, last, last, last), (0, 6, 11, 16, last, last, last, last, last))

    def kernel(dg_ref, du_ref, gate_ref, up_ref, *refs):
        ins, o_ref, outs, (acc, *scratch) = refs[:n], refs[n], refs[n + 1 : 2 * n + 1], refs[2 * n + 1 :]
        at = Place()
        tasks = sums_of(at, n, ins, outs, scratch)
        now = pl.program_id(0)

        @pl.when(now == 0)
        def _():
            meet(neighbours(at, True))

        beside(tasks, steps[:n])
        for i in range(tokens // ROWS):
            r = pl.ds(i * ROWS, ROWS)
            part = dot_nt_f32(dg_ref[r], gate_ref[...]) + dot_nt_f32(du_ref[r], up_ref[...])

            @pl.when(now == 0)
            def _():
                acc[r] = part

            @pl.when(now > 0)
            def _():
                acc[r] += part

        @pl.when(now == last)
        def _():
            o_ref[...] = acc[...].astype(BF16)

    outs = pl.pallas_call(
        kernel,
        grid=(last + 1,),
        out_shape=[jax.ShapeDtypeStruct((tokens, d), BF16)] + [jax.ShapeDtypeStruct(t.shape[3:], BF16) for t in shaped],
        in_specs=[column_block(tokens)] * 2 + [column_block(d)] * 2 + [ANY] * n,
        out_specs=[pl.BlockSpec((tokens, d), lambda j: (0, 0), pipeline_mode=pl.Buffered(1))] + [WHOLE] * n,
        scratch_shapes=[pltpu.VMEM((tokens, d), F32)] + [one for t in shaped for one in sum_scratch(*t.shape[3:])],
        compiler_params=params(collective_id),
        cost_estimate=cost(3, 80),
        name="back_up",
    )(dg, du, gate, up, *shaped)
    return outs[0], outs[1:]


def solution(mesh):
    def fetched(w):
        return lax.all_gather(w, "s", axis=0, tiled=True)

    def scattered(term):
        return lax.psum(lax.psum_scatter(term, "s", scatter_dimension=0, tiled=True), "r")

    def step(x, dy, w_gate, w_up, w_down):
        x, dy = x[0], dy[0]
        down0, down1 = fetched(w_down[0]), fetched(w_down[1])
        gate0, up0 = gathered(w_gate[0], w_up[0], collective_id=1)

        a0, back_norm0 = jax.vjp(normed, x)
        (g0, u0, m0), (gate1, up1) = gate_up(a0, gate0, up0, (w_gate[1], w_up[1]), 2)
        h1 = x + matmul(m0, down0)
        a1, back_norm1 = jax.vjp(normed, h1)
        m1, dg1, du1 = middle(a1, dy, gate1, up1, down1)
        by_down1 = scattered(dot_tn(m1, dy))
        by_gate1 = scattered(dot_tn(a1, dg1))
        by_up1 = scattered(dot_tn(a1, du1))
        by_h1 = dy + back_norm1(dot_nt(dg1, gate1) + dot_nt(du1, up1))[0]

        (dg0, du0), (by_down0,) = back_down(by_h1, down0, g0, u0, (dot_tn(m0, by_h1),), 3)
        by_a0, (by_gate0, by_up0) = back_up(dg0, du0, gate0, up0, (dot_tn(a0, dg0), dot_tn(a0, du0)), 4)
        by_x = by_h1 + back_norm0(by_a0)[0]
        return by_x[None], jnp.stack([by_gate0, by_gate1]), jnp.stack([by_up0, by_up1]), jnp.stack([by_down0, by_down1])

    states, cut = P(("rep", "r", "s"), None, None), P(None, "s", None)
    return jax.shard_map(
        step,
        mesh=mesh,
        in_specs=(states, states) + (cut,) * 3,
        out_specs=(states,) + (P("rep", "s", None),) * 3,
        check_vma=False,
    )
```

time: 1020 us -> 891 us (0.87)
  Pallas kernels: 158 us -> 509 us
  matrix products: 592 us -> 277 us
  waiting for transfers between devices: 182 us -> 38.1 us
  local copies, waits for them, and re-layouts: 30.7 us -> 7.4 us
    pallas_call x1 -> x5, Pallas kernels: 158 us -> 509 us  [the longest x1 139 us: back_up(): pl.pallas_call(kernel, grid=(last + 1,), out_shape=[jax.ShapeDtypeStruct(...]
    all_gather x6 -> x2, waiting for transfers between devices: 180 us -> 0.02 us  [fetched(): return lax.all_gather(w, 's', axis=0, tiled=True)]
    dot_general x4 -> x0, matrix products: 166 us -> none  [dot_f32(): return jnp.dot(a, w, preferred_element_type=F32)]
    dot_general x6 -> x2, matrix products: 205 us -> 62.9 us  [dot_nt(): lax.dot_general(a, w, (((1,), (1,)), ((), ())), preferred_element_type=F32)]
    psum x1, waiting for transfers between devices: 0.02 us -> 37.2 us  [scattered(): lax.psum(lax.psum_scatter(term, 's', scatter_dimension=0, tiled=True), 'r')]
    unnamed x25 -> x28, local copies, waits for them, and re-layouts: 24.8 us -> 2.95 us
  transfers between devices with their start and end apart: 10 -> 6, of which waited for: 6 -> 1; matrix products, arithmetic and copies ran while one was open for 55% -> 32% of each run, Pallas kernels for 16% -> 48%
where the time goes in v2:
time: 891 us; the launch traced here: 887 us
  Pallas kernels  509 us (57%)
  matrix products  277 us (31%)
  other arithmetic  40.7 us (5%)
  waiting for transfers between devices  38.1 us (4%)
  between operations  14.5 us (2%)
    dot_general x6, matrix products, dot_tn(): lax.dot_general(a, w, (((0,), (0,)), ((), ())), preferred_element_type=F32)  184 us
    pallas_call x1, Pallas kernels, back_up(): pl.pallas_call(kernel, grid=(last + 1,), out_shape=[jax.ShapeDtypeStruct(...  139 us
    pallas_call x1, Pallas kernels, gathered(): pl.pallas_call(kernel, out_shape=[whole_shape(b) for b in blocks], in_spe...  99.9 us
    pallas_call x1, Pallas kernels, gate_up(): pl.pallas_call(kernel, grid=(last + 1,), out_shape=[jax.ShapeDtypeStruct(...  97 us
    pallas_call x1, Pallas kernels, back_down(): pl.pallas_call(kernel, grid=(last + 1,), out_shape=[jax.ShapeDtypeStruct(...  93.4 us
    pallas_call x1, Pallas kernels, middle(): pl.pallas_call(kernel, grid=(hidden // TILE,), out_shape=[jax.ShapeDtypeS...  80.4 us
    dot_general x2, matrix products, dot_nt(): lax.dot_general(a, w, (((1,), (1,)), ((), ())), preferred_element_type=F32)  62.9 us
    psum x1, waiting for transfers between devices, scattered(): lax.psum(lax.psum_scatter(term, 's', scatter_dimension=0, tiled=True), 'r')  37.2 us
  transfers between devices with their start and end apart: 6, of which 1 were waited for; matrix products, arithmetic and copies ran while one was open for 32% of the time, Pallas kernels for 48%

profile of v2, /device:TPU:0, one launch (start us, length us, event | category | flops | bytes accessed | tf_op | source)
XLA Modules:
  0.0 887.1 jit_solution(15315511354846986749)
XLA Ops:
  7.2 0.0 all-gather.5.cloned.1.call-start
  7.2 2.0 fusion.19
  9.2 0.0 all-gather.5.cloned.1.call-update
  9.3 0.0 all-gather.7.cloned.1.call-start
  9.3 0.7 all-gather.7.cloned.1.call-update
  10.0 0.0 reduce-scatter.8.cloned.1.call-start
  10.1 0.0 copy-start
  10.1 3.7 fusion.4
  13.8 0.6 copy-done.5
  14.4 2.4 slice_bitcast_fusion
  16.8 0.0 copy-done
  16.8 3.3 fusion.5.a_ref
  20.1 0.0 copy-done.7
  20.1 99.9 %gathered.1 = (bf16[4,4,2,40,4352]{4,3,2,1,0:T(8,128)(2,1)}, bf16[4,4,2,40,4352]{4,3,2,1,0:T(8,128)(2,1)}) custom-call(bf16[40,4352]{1,0:T(8,128)(2,1)} %get-tuple-element.49.refs_0_, bf16[40,4352]{1,0:T(8,128)(2,1)} %get-tuple-element.42.refs_1_), custom_call_target="tpu_custom_call" | custom-call | flops 68451041280 | bytes 31457280 | tf_op jit(solution)/shard_map/gathered/pallas_call | solution.py:321
  120.0 97.0 %gate_up.1 = (f32[2048,4352]{1,0:T(8,128)}, f32[2048,4352]{1,0:T(8,128)}, bf16[2048,4352]{1,0:T(8,128)(2,1)}, bf16[4,4,2,40,4352]{4,3,2,1,0:T(8,128)(2,1)}, bf16[4,4,2,40,4352]{4,3,2,1,0:T(8,128)(2,1)}) custom-call(bf16[2048,1280]{1,0:T(8,128)(2,1)} %fusion.5.a_ref, bf16[1280,4352]{1,0:T(8,128)(2,1)} %bitcast.64, bf16[1280,4352]{1,0:T(8,128)(2,1)} %bitcast.66, ...), custom_call_target="tpu_custom_call" | custom-call | flops 45634027520 | bytes 115343360 | tf_op jit(solution)/shard_map/gate_up/pallas_call | solution.py:411
  217.0 0.0 all-gather.5.cloned.1.call-done
  217.0 30.1 %fusion.7 = (f32[2048]{0:T(1024)S(1)}, bf16[2048,1280]{1,0:T(8,128)(2,1)S(1)}) fusion(bf16[2048,4352]{1,0:T(8,128)(2,1)} %get-tuple-element.22, bf16[1,4352,1280]{2,1,0:T(8,128)(2,1)} %all-gather.5.cloned.1.call-done, bf16[1,2048,1280]{2,1,0:T(8,128)(2,1)} %param.5), kind=kOutput, calls=%fused_computation.23 | convolution fusion | flops 22830118912 | bytes 39460864 | tf_op jit(solution)/shard_map/dot_general | solution.py:16
  247.1 0.0 copy-start.11
  247.1 0.0 copy-start.1
  247.1 0.6 copy-done.11
  247.7 1.7 copy-done.1
  249.4 0.0 copy-done.9
  249.4 3.4 fusion.8.a_ref
  252.8 80.4 %middle.1 = (bf16[2048,4352]{1,0:T(8,128)(2,1)}, bf16[2048,4352]{1,0:T(8,128)(2,1)}, bf16[2048,4352]{1,0:T(8,128)(2,1)}) custom-call(bf16[2048,1280]{1,0:T(8,128)(2,1)} %fusion.8.a_ref, bf16[2048,1280]{1,0:T(8,128)(2,1)} %bitcast.55, bf16[1280,4352]{1,0:T(8,128)(2,1)} %bitcast.68, bf16[1280,4352]{1,0:T(8,128)(2,1)} %bitcast.70, bf16[4352,1280]{1,0:T(8,128)(2,1)} %bitcast.63), custom_call_target="tpu_custom_call" | custom-call | flops 68451041280 | bytes 104857600 | tf_op jit(solution)/shard_map/middle/pallas_call | solution.py:437
  333.2 30.2 %convolution_convert_fusion.4 = bf16[4352,1280]{1,0:T(8,128)(2,1)} fusion(bf16[2048,4352]{1,0:T(8,128)(2,1)} %get-tuple-element.35, bf16[1,2048,1280]{2,1,0:T(8,128)(2,1)} %param.6), kind=kOutput, calls=%fused_computation.4 | convolution fusion | flops 22822584320 | bytes 34209792 | tf_op jit(solution)/shard_map/dot_general | solution.py:28
  363.4 0.0 reduce-scatter.8.cloned.1.call-update
  363.4 0.0 reduce-scatter.6.cloned.1.call-start
  363.5 31.3 %convolution_convert_fusion = bf16[1280,4352]{1,0:T(8,128)(2,1)} fusion(bf16[2048,1280]{1,0:T(8,128)(2,1)} %fusion.8.a_ref, bf16[2048,4352]{1,0:T(8,128)(2,1)} %get-tuple-element.26), kind=kOutput, calls=%fused_computation | convolution fusion | flops 22822584320 | bytes 34209792 | tf_op jit(solution)/shard_map/dot_general | solution.py:28
  394.8 0.0 reduce-scatter.6.cloned.1.call-update
  394.8 0.0 reduce-scatter.4.cloned.1.call-start
  394.8 30.8 %convolution_convert_fusion.6 = bf16[2048,1280]{1,0:T(8,128)(2,1)} fusion(bf16[2048,4352]{1,0:T(8,128)(2,1)} %get-tuple-element.26, bf16[1280,4352]{1,0:T(8,128)(2,1)} %bitcast.71), kind=kOutput, calls=%fused_computation.26 | convolution fusion | flops 22819635200 | bytes 34209792 | tf_op jit(solution)/shard_map/dot_general | solution.py:24
  425.7 32.1 %fusion.9 = (f32[2048]{0:T(1024)S(1)}, bf16[2048,1280]{1,0:T(8,128)(2,1)}) fusion(bf16[2048,1280]{1,0:T(8,128)(2,1)} %copy-done.1, bf16[2048,1280]{1,0:T(8,128)(2,1)} %convolution_convert_fusion.6, bf16[2048,4352]{1,0:T(8,128)(2,1)} %get-tuple-element.25, bf16[1280,4352]{1,0:T(8,128)(2,1)} %bitcast.69), kind=kOutput, calls=%fused_computation.25 | convolution fusion | flops 22832740352 | bytes 44703744 | tf_op jit(solution)/shard_map/dot_general | solution.py:24
  457.8 0.0 copy-done.12
  457.8 0.0 copy-done.10
  457.8 9.5 %fusion.14.dy_ref = bf16[2048,1280]{1,0:T(8,128)(2,1)} fusion(bf16[2048,1280]{1,0:T(8,128)(2,1)} %copy-done.1, bf16[2048,1280]{1,0:T(8,128)(2,1)} %get-tuple-element.48, f32[2048]{0:T(1024)S(1)} %multiply_multiply_fusion.1, f32[2048]{0:T(1024)S(1)} %copy-done.10, bf16[1,2048,1280]{2,1,0:T(8,128)(2,1)} %param.6), kind=kLoop, calls=%fused_computation.33 | loop fusion | flops 18350080 | bytes 20987904 | tf_op jit(solution)/shard_map/add | solution.py:553
  467.3 31.5 %convolution_convert_fusion.1 = bf16[1280,4352]{1,0:T(8,128)(2,1)} fusion(bf16[2048,1280]{1,0:T(8,128)(2,1)} %fusion.8.a_ref, bf16[2048,4352]{1,0:T(8,128)(2,1)} %get-tuple-element.25), kind=kOutput, calls=%fused_computation.1 | convolution fusion | flops 22822584320 | bytes 34209792 | tf_op jit(solution)/shard_map/dot_general | solution.py:28
  498.8 30.0 %convolution_convert_fusion.5 = bf16[4352,1280]{1,0:T(8,128)(2,1)} fusion(bf16[2048,4352]{1,0:T(8,128)(2,1)} %get-tuple-element.22, bf16[2048,1280]{1,0:T(8,128)(2,1)} %fusion.14.dy_ref), kind=kOutput, calls=%fused_computation.5 | convolution fusion | flops 22822584320 | bytes 34209792 | tf_op jit(solution)/shard_map/dot_general | solution.py:28
  528.8 0.0 reduce-scatter.4.cloned.1.call-update
  528.8 0.0 all-reduce.3.cloned.1.call-start
  528.9 93.4 %back_down.1 = (bf16[2048,4352]{1,0:T(8,128)(2,1)}, bf16[2048,4352]{1,0:T(8,128)(2,1)}, bf16[136,1280]{1,0:T(8,128)(2,1)}) custom-call(bf16[2048,1280]{1,0:T(8,128)(2,1)} %fusion.14.dy_ref, bf16[4352,1280]{1,0:T(8,128)(2,1)} %bitcast.62, f32[2048,4352]{1,0:T(8,128)} %get-tuple-element.27.g_ref, f32[2048,4352]{1,0:T(8,128)} %get-tuple-element.28.u_ref, ...), custom_call_target="tpu_custom_call" | custom-call | flops 45634027520 | bytes 125829120 | tf_op jit(solution)/shard_map/back_down/pallas_call | solution.py:471
  622.3 0.0 copy-start.13
  622.3 31.5 %convolution_convert_fusion.3 = bf16[1280,4352]{1,0:T(8,128)(2,1)} fusion(bf16[2048,1280]{1,0:T(8,128)(2,1)} %fusion.5.a_ref, bf16[2048,4352]{1,0:T(8,128)(2,1)} %get-tuple-element.29.dg_ref), kind=kOutput, calls=%fused_computation.3 | convolution fusion | flops 22822584320 | bytes 34209792 | tf_op jit(solution)/shard_map/dot_general | solution.py:28
  653.8 0.0 copy-done.13
  653.8 29.4 %convolution_convert_fusion.2 = bf16[1280,4352]{1,0:T(8,128)(2,1)} fusion(bf16[2048,1280]{1,0:T(8,128)(2,1)} %fusion.5.a_ref, bf16[2048,4352]{1,0:T(8,128)(2,1)S(1)} %copy-done.13), kind=kOutput, calls=%fused_computation.2 | convolution fusion | flops 22822584320 | bytes 34209792 | tf_op jit(solution)/shard_map/dot_general | solution.py:28
  683.2 138.6 %back_up.1 = (bf16[2048,1280]{1,0:T(8,128)(2,1)}, bf16[40,4352]{1,0:T(8,128)(2,1)}, bf16[40,4352]{1,0:T(8,128)(2,1)}) custom-call(bf16[2048,4352]{1,0:T(8,128)(2,1)} %get-tuple-element.29.dg_ref, bf16[2048,4352]{1,0:T(8,128)(2,1)} %get-tuple-element.30.du_ref, bf16[1280,4352]{1,0:T(8,128)(2,1)} %bitcast.65, bf16[1280,4352]{1,0:T(8,128)(2,1)} %bitcast.67, ...), custom_call_target="tpu_custom_call" | custom-call | flops 68451041280 | bytes 83886080 | tf_op jit(solution)/shard_map/back_up/pallas_call | solution.py:519
  821.8 0.0 copy-start.6
  821.8 0.0 copy-start.8
  821.9 5.5 fusion.6
  827.4 0.0 copy-done.6
  827.4 0.0 reduce-scatter.8.cloned.1.call-done
  827.4 0.0 reduce-scatter.6.cloned.1.call-done
  827.4 0.0 reduce-scatter.4.cloned.1.call-done
  827.5 0.0 all-reduce.3.cloned.1.call-update
  827.5 0.0 copy-done.8
  827.5 0.0 copy-start.4
  827.5 0.0 copy-start.3
  827.5 9.6 %fusion.13 = bf16[1,2048,1280]{2,1,0:T(8,128)(2,1)} fusion(bf16[2048,1280]{1,0:T(8,128)(2,1)} %fusion.14.dy_ref, bf16[2048,1280]{1,0:T(8,128)(2,1)} %get-tuple-element.31, bf16[1,2048,1280]{2,1,0:T(8,128)(2,1)} %param.5, f32[2048]{0:T(1024)S(1)} %multiply_multiply_fusion, f32[2048]{0:T(1024)S(1)} %copy-done.8), kind=kLoop, calls=%fused_computation.32 | loop fusion | flops 18350080 | bytes 20987904 | tf_op jit(solution)/shard_map/broadcast_in_dim | solution.py:558
  837.1 37.2 %all-reduce.3.cloned.1.call-done = (bf16[1,40,4352]{2,1,0:T(8,128)(2,1)}, bf16[1,40,4352]{2,1,0:T(8,128)(2,1)}, bf16[1,136,1280]{2,1,0:T(8,128)(2,1)}) async-done(((bf16[1,40,4352]{2,1,0:T(8,128)(2,1)}, bf16[1,40,4352]{2,1,0:T(8,128)(2,1)}, bf16[1,136,1280]{2,1,0:T(8,128)(2,1)}), (bf16[1,40,4352]{2,1,0:T(8,128)(2,1)}, bf16[1,40,4352]{2,1,0:T(8,128)(2,1)}, ...) | async-done | bytes 1044496 | tf_op jit(solution)/shard_map/psum | solution.py:538
  874.4 0.0 copy-done.4
  874.4 1.9 pad_maximum_fusion
  876.2 0.0 copy-done.3
  876.3 1.9 pad_maximum_fusion.1
  878.1 0.0 copy-done.2
  878.1 1.9 pad_maximum_fusion.2
  (11 shorter events, 0.0 us)
Async XLA Ops:
  7.2 209.8 %all-gather.5.cloned.1.call-start = ((), (), s32[]{:S(2)}) async-start(), calls=%async_computation.6 | async-start | bytes 11489280 | tf_op jit(solution)/shard_map/all_gather | solution.py:535
  9.3 243.5 %all-gather.7.cloned.1.call-start = ((), (), s32[]{:S(2)}) async-start(), calls=%async_computation.7 | async-start | bytes 11489280 | tf_op jit(solution)/shard_map/all_gather | solution.py:535
  10.0 817.4 %reduce-scatter.8.cloned.1.call-start = ((), (), s32[]{:S(2)}) async-start(), calls=%async_computation.5 | async-start | bytes 11489280 | tf_op jit(solution)/shard_map/reduce_scatter | solution.py:538
  10.1 6.8 copy-start
  13.8 0.6 copy-start.5
  14.4 5.7 copy-start.7
  247.1 0.6 copy-start.11
  247.1 2.3 copy-start.1
  247.7 1.7 copy-start.9
  363.4 464.0 %reduce-scatter.6.cloned.1.call-start = ((), (), s32[]{:S(2)}) async-start(), calls=%async_computation.4 | async-start | bytes 11489280 | tf_op jit(solution)/shard_map/reduce_scatter | solution.py:538
  394.8 432.7 %reduce-scatter.4.cloned.1.call-start = ((), (), s32[]{:S(2)}) async-start(), calls=%async_computation.3 | async-start | bytes 11489280 | tf_op jit(solution)/shard_map/reduce_scatter | solution.py:538
  425.7 32.1 %copy-start.12 = (f32[2048]{0:T(1024)S(1)}, f32[2048]{0:T(1024)}, u32[]{:S(2)}) copy-start(f32[2048]{0:T(1024)} %copy-done.11) | copy-start | bytes 24580
  425.7 32.2 %copy-start.10 = (f32[2048]{0:T(1024)S(1)}, f32[2048]{0:T(1024)}, u32[]{:S(2)}) copy-start(f32[2048]{0:T(1024)} %copy-done.9) | copy-start | bytes 24580
  528.8 345.5 %all-reduce.3.cloned.1.call-start = ((), (), s32[]{:S(2)}) async-start(), calls=%async_computation.8 | async-start | bytes 2088960 | tf_op jit(solution)/shard_map/psum | solution.py:538
  622.3 31.5 %copy-start.13 = (bf16[2048,4352]{1,0:T(8,128)(2,1)S(1)}, bf16[2048,4352]{1,0:T(8,128)(2,1)}, u32[]{:S(2)}) copy-start(bf16[2048,4352]{1,0:T(8,128)(2,1)} %get-tuple-element.30.du_ref) | copy-start | bytes 53477380
  821.8 5.5 copy-start.6
  821.8 5.6 copy-start.8
  827.5 46.9 %copy-start.4 = (bf16[40,4352]{1,0:T(8,128)(2,1)S(1)}, bf16[40,4352]{1,0:T(8,128)(2,1)}, u32[]{:S(2)}) copy-start(bf16[40,4352]{1,0:T(8,128)(2,1)} %get-tuple-element.32) | copy-start | bytes 1044484
  827.5 48.7 %copy-start.3 = (bf16[40,4352]{1,0:T(8,128)(2,1)S(1)}, bf16[40,4352]{1,0:T(8,128)(2,1)}, u32[]{:S(2)}) copy-start(bf16[40,4352]{1,0:T(8,128)(2,1)} %get-tuple-element.33) | copy-start | bytes 1044484
  827.5 50.6 %copy-start.2 = (bf16[136,1280]{1,0:T(8,128)(2,1)S(1)}, bf16[136,1280]{1,0:T(8,128)(2,1)}, u32[]{:S(2)}) copy-start(bf16[136,1280]{1,0:T(8,128)(2,1)} %get-tuple-element.34) | copy-start | bytes 1044484
Sparse Core Ops, SparseCore 0:
  10.3 78.6 all-gather.4
  91.3 82.7 all-gather.6
  363.5 96.4 reduce-scatter.7
  463.7 100.1 reduce-scatter.5
  567.7 97.4 reduce-scatter.3
  827.6 46.7 all-reduce.2
